TPU v7x, 256 devices: a whole 4x4x8 slice. The times are simulated.
256 devices in a mesh: rows: 32 (over y, z), cols: 8 (over x, core).
Axes of the slice: x: 4, y: 4, z: 8, core: 2. Of those that a mesh axis runs over, the one named last changes fastest.
Arguments:
- token_ids: int32 [128, 256], P('rows'), may hold values from 0 to 8191
- keep_mask: int32 [128, 256], P('rows'), may hold values 0 or 1
- remask_order: int32 [32768], P('rows'), may hold values from 0 to 32767, each once
- embed_table: bfloat16 [8192, 1024], P(None, 'cols'), may hold values from -6 to 6
- mask_embed: bfloat16 [1024], P('cols'), may hold values from -4 to 4
- conv_one: bfloat16 [3, 3, 1024, 1024], P(None, None, None, 'cols'), may hold values from -0.0625 to 0.0625
- gain_one: float32 [1024], P('cols'), may hold values from 0.25 to 1.75
- bias_one: float32 [1024], P('cols'), may hold values from -3 to 3
- conv_two: bfloat16 [3, 3, 1024, 1024], P(None, None, None, 'cols'), may hold values from -0.0625 to 0.0625
- gain_two: float32 [1024], P('cols'), may hold values from 0.25 to 1.75
- bias_two: float32 [1024], P('cols'), may hold values from -3 to 3
- head_weight: bfloat16 [1024, 8192], P(None, 'cols'), may hold values from -15.6 to 15.6
Outputs:
- features: bfloat16 [128, 256, 1024], P('rows', None, 'cols')
- token_logp: float32 [128, 256], P('rows', 'cols')
Inputs may be any that keep to these rules, and one draw needn't show every extreme that they name: `remask_order`: each rank appears once.
All inputs are finite; a program needn't handle non-finite values. No bound on the sum of `keep_mask` on one device may be relied on, other than what follows from the above.
Results may differ from a plain program's by a relative error of at most 0.0039.
Values may be sent and summed in bfloat16 or wider, within the bound.
A program may use at most 128 MiB of HBM per device.

v0:
```python
import jax
import jax.numpy as jnp
from jax import lax
from jax.sharding import PartitionSpec as P

C = 1024
GROUPS = 32


def with_halo(value, sides, width):
    for axis, dim in sides:
        count, length = (lax.axis_size(axis), value.shape[dim])
        up = [(i, (i + 1) % count) for i in range(count - 1)]
        down = [(j, i) for i, j in up]
        last = lax.slice_in_dim(value, length - width, length, axis=dim)
        leading = lax.slice_in_dim(value, 0, width, axis=dim)
        before = lax.ppermute(last, axis, up)
        after = lax.ppermute(leading, axis, down)
        value = jnp.concatenate([before, value, after], axis=dim)
    return value


def sent_to_all(value, axis):
    copies = jnp.broadcast_to(value, (lax.axis_size(axis), *value.shape))
    return lax.all_to_all(copies, axis, split_axis=0, concat_axis=0, tiled=True)


def over_copies(value, axis):
    return sent_to_all(value, axis).sum(axis=0)


def together(arrays, axis):
    ends = [0]
    for a in arrays:
        ends.append(ends[-1] + a.size)
    so_far = over_copies(jnp.concatenate([a.ravel() for a in arrays]), axis)
    return tuple((so_far[b:e].reshape(a.shape) for a, b, e in zip(arrays, ends, ends[1:])))


def laid_out(tiles, dim):
    tiles = jnp.moveaxis(tiles, 0, dim)
    lengths = tiles.shape
    return tiles.reshape(*lengths[:dim], lengths[dim] * lengths[dim + 1], *lengths[dim + 2 :])


def gathered_copies(value, axis, dim):
    tiles = sent_to_all(value, axis)
    return laid_out(tiles, dim)


def all_in_one(value, axis):
    leaves = jax.tree.leaves(value)
    order = sorted(range(len(leaves)), key=lambda k: -leaves[k].size)
    width = (1, *leaves[order[0]].shape)[-1]
    lines = [
        jnp.pad(leaves[k].reshape(-1), (0, -leaves[k].size % width)).reshape(-1, width)
        for k in order
    ]
    both, at, found = (sent_to_all(jnp.concatenate(lines), axis), 0, {})
    for k, line in zip(order, lines):
        section = both[:, at : at + len(line)].reshape(len(both), -1)
        found[k] = section[:, : leaves[k].size].reshape(-1, *leaves[k].shape)
        at += len(line)
    numbers = iter(range(len(leaves)))
    return jax.tree.map(lambda _: found[next(numbers)], value)


def folded_in_pairs(pieces, combine):
    while len(jax.tree.leaves(pieces)[0]) > 1:
        pieces = jax.vmap(combine)(
            *(jax.tree.map(lambda part: part[side::2], pieces) for side in (0, 1))
        )
    return jax.tree.map(lambda part: part[0], pieces)


def joined_all(value, axis, combine):
    pieces = all_in_one(value, axis)
    return folded_in_pairs(pieces, combine)


def add_taps(total, weight, piece):
    rows_here = piece.shape[0] - 2
    width = piece.shape[1]
    count = piece.shape[2]
    padded = jnp.pad(piece, ((0, 0), (1, 1), (0, 0)))
    for shift_row in range(3):
        for shift_col in range(3):
            window = padded[
                shift_row : shift_row + rows_here, shift_col : shift_col + width
            ].reshape(-1, count)
            taps = weight[shift_row, shift_col]
            total = total + jnp.dot(window, taps, preferred_element_type=jnp.float32)
    return total


def convolve(field, weight):
    rows_here, width, _ = field.shape
    empty = jnp.zeros((rows_here * width, weight.shape[3]), jnp.float32)
    rimmed = with_halo(field, (("rows", 0),), 1)
    total = add_taps(empty, weight, lax.all_gather(rimmed, "cols", axis=2, tiled=True))
    return total.reshape(rows_here, width, -1)


def group_norm(values, gain, bias, height):
    rows_here, width, channels = values.shape
    group_width = C // GROUPS
    flat = values.reshape(rows_here * width, channels // group_width, group_width)
    population = height * width * group_width
    sums, squares = together(
        (jnp.sum(flat, axis=(0, 2)), jnp.sum(flat * flat, axis=(0, 2))), "rows"
    )
    mean = sums / population
    variance = squares / population - mean * mean
    deviation = flat - mean[None, :, None]
    normed = deviation / jnp.sqrt(variance + 1e-05)[None, :, None]
    return normed.reshape(rows_here, width, channels) * gain + bias


def combine_totals(first, second):
    top = jnp.maximum(first[0], second[0])
    summed = first[1] * jnp.exp(first[0] - top) + second[1] * jnp.exp(second[0] - top)
    return (top, summed, first[2] + second[2])


def local(
    token_ids,
    keep_mask,
    remask_order,
    embed_table,
    mask_embed,
    conv_one,
    gain_one,
    bias_one,
    conv_two,
    gain_two,
    bias_two,
    head_weight,
):
    rows_here, width = token_ids.shape
    height = rows_here * lax.axis_size("rows")
    num_cols = lax.axis_size("cols")
    order = remask_order.reshape(rows_here, width)
    visible = (keep_mask == 1) | (order >= height * width // 2)
    looked = jnp.take(embed_table, token_ids, axis=0)
    start = jnp.where(visible[:, :, None], looked, mask_embed[None, None, :])
    hidden = jax.nn.silu(group_norm(convolve(start, conv_one), gain_one, bias_one, height)).astype(
        jnp.bfloat16
    )
    second = group_norm(convolve(hidden, conv_two), gain_two, bias_two, height)
    features = (start.astype(jnp.float32) + second).astype(jnp.bfloat16)
    vocab_here = head_weight.shape[1]
    piece = gathered_copies(features, "cols", 2)
    count = piece.shape[2]
    logits = jnp.dot(piece.reshape(-1, count), head_weight, preferred_element_type=jnp.float32)
    top = jnp.max(logits, axis=1)
    summed = jnp.sum(jnp.exp(logits - top[:, None]), axis=1)
    offset = lax.axis_index("cols") * vocab_here
    vocab_ids = lax.broadcasted_iota(jnp.int32, (1, vocab_here), 1) + offset
    hits = vocab_ids == token_ids.reshape(-1, 1)
    picked = jnp.sum(jnp.where(hits, logits, 0.0), axis=1)
    top, summed, picked = joined_all((top, summed, picked), "cols", combine_totals)
    logp = (picked - top - jnp.log(summed)).reshape(rows_here, width)
    slice_width = width // num_cols
    token_logp = lax.dynamic_slice_in_dim(
        logp, lax.axis_index("cols") * slice_width, slice_width, 1
    )
    return (features, token_logp)


def solution(mesh):
    in_specs = (
        P("rows", None),
        P("rows", None),
        P("rows"),
        P(None, "cols"),
        P("cols"),
        P(None, None, None, "cols"),
        P("cols"),
        P("cols"),
        P(None, None, None, "cols"),
        P("cols"),
        P("cols"),
        P(None, "cols"),
    )
    out_specs = (P("rows", None, "cols"), P("rows", "cols"))
    return jax.shard_map(local, mesh=mesh, in_specs=in_specs, out_specs=out_specs, check_vma=False)
```

profile of v0, /device:TPU:1, one launch (start us, length us, event | category | flops | bytes accessed | tf_op | source)
XLA Modules:
  0.0 250.8 jit_solution(9500933285625379632)
XLA Ops:
  7.2 0.8 broadcast_compare_fusion
  8.1 0.7 fusion.46
  8.8 0.7 compare_and_fusion
  9.5 4.7 %gather_fusion = bf16[1024,128]{1,0:T(8,128)(2,1)S(1)} fusion(bf16[8192,128]{1,0:T(8,128)(2,1)} %param.15, s32[1024]{0:T(1024)S(1)} %broadcast_clamp_fusion), kind=kCustom, calls=%fused_computation | custom fusion | bytes 528384 | tf_op jit(solution)/shard_map/jit(_take)/gather | solution.py:144
  14.2 0.3 select_select_fusion
  14.6 4.4 %collective-permute-start = (bf16[1,256,128]{2,1,0:T(8,128)(2,1)S(1)}, bf16[1,256,128]{2,1,0:T(8,128)(2,1)S(1)}, u32[]{:S(2)}, u32[]{:S(2)}) collective-permute-start(bf16[1,256,128]{2,1,0:T(8,128)(2,1)S(1)} %get-tuple-element.32), channel_id=1, source_target_pairs={{0,8},{8,16},{16,24},{24,32},{32,40},{40,48},{48,56},{56,64},{64,7... | collective-permute-start | bytes 196616 | tf_op jit(solution)/shard_map/ppermute | solution.py:17
  19.0 1.3 collective-permute-start.1
  20.3 3.9 %collective-permute-done.1 = bf16[1,256,128]{2,1,0:T(8,128)(2,1)S(1)} collective-permute-done((bf16[1,256,128]{2,1,0:T(8,128)(2,1)S(1)}, bf16[1,256,128]{2,1,0:T(8,128)(2,1)S(1)}, u32[]{:S(2)}, u32[]{:S(2)}) %collective-permute-start.1) | collective-permute-done | bytes 65568 | tf_op jit(solution)/shard_map/ppermute | solution.py:18
  24.2 0.8 pad_maximum_fusion
  25.0 38.2 %all-gather.3.cloned.1.call-done = bf16[6,256,1024]{2,1,0:T(8,128)(2,1)} async-done(((bf16[6,256,128]{2,1,0:T(8,128)(2,1)}), bf16[6,256,1024]{2,1,0:T(8,128)(2,1)}) %all-gather.3.cloned.1.call-update) | async-done | bytes 3145744 | tf_op jit(solution)/shard_map/all_gather | solution.py:100
  63.3 13.0 %pad_slice_fusion.6 = (bf16[4,256,1024]{2,1,0:T(8,128)(2,1)S(1)}, bf16[4,256,1024]{2,1,0:T(8,128)(2,1)}, bf16[4,256,1024]{2,1,0:T(8,128)(2,1)}, bf16[4,256,1024]...) fusion(bf16[6,256,1024]{2,1,0:T(8,128)(2,1)} %all-gather.3.clon, ...), kind=kLoop, calls=%fused_computation.12 | loop fusion | bytes 28311552 | tf_op jit(solution)/shard_map/slice | solution.py:88
  76.3 1.8 fusion.21
  78.1 1.8 convolution_add_fusion.15
  79.9 1.8 convolution_add_fusion.14
  81.8 0.7 convolution_add_fusion.13
  82.5 0.7 convolution_add_fusion.12
  83.2 0.7 convolution_add_fusion.11
  84.0 0.7 convolution_add_fusion.10
  84.7 0.7 convolution_add_fusion.9
  85.5 0.7 fusion.48
  86.7 18.0 %all_to_all.22 = f32[32,1,8]{2,1,0:T(1,128)S(1)} all-to-all(f32[32,1,8]{2,1,0:T(1,128)S(1)} %broadcast_in_dim.60), channel_id=1, replica_groups=mesh['rows'=32,'cols'=8] {'rows'}, dimensions={0} | all-to-all | bytes 2048 | tf_op jit(solution)/shard_map/all_to_all | solution.py:25
  105.5 2.2 collective-permute-start.2
  107.7 1.5 collective-permute-start.3
  109.2 3.5 %collective-permute-done.3 = bf16[1,256,128]{2,1,0:T(8,128)(2,1)S(1)} collective-permute-done((bf16[1,256,128]{2,1,0:T(8,128)(2,1)S(1)}, bf16[1,256,128]{2,1,0:T(8,128)(2,1)S(1)}, u32[]{:S(2)}, u32[]{:S(2)}) %collective-permute-start.3) | collective-permute-done | bytes 65568 | tf_op jit(solution)/shard_map/ppermute | solution.py:18
  112.7 0.8 pad_maximum_fusion.1
  113.5 35.7 %all-gather.5.cloned.1.call-done = bf16[6,256,1024]{2,1,0:T(8,128)(2,1)} async-done(((bf16[6,256,128]{2,1,0:T(8,128)(2,1)}), bf16[6,256,1024]{2,1,0:T(8,128)(2,1)}) %all-gather.5.cloned.1.call-update) | async-done | bytes 3145744 | tf_op jit(solution)/shard_map/all_gather | solution.py:100
  149.2 13.0 %pad_slice_fusion = (bf16[4,256,1024]{2,1,0:T(8,128)(2,1)S(1)}, bf16[4,256,1024]{2,1,0:T(8,128)(2,1)}, bf16[4,256,1024]{2,1,0:T(8,128)(2,1)}, bf16[4,256,1024]{2...) fusion(bf16[6,256,1024]{2,1,0:T(8,128)(2,1)} %all-gather.5.clon, ...), kind=kLoop, calls=%fused_computation.6 | loop fusion | bytes 28311552 | tf_op jit(solution)/shard_map/slice | solution.py:88
  162.2 1.8 fusion.11
  164.0 1.8 convolution_add_fusion.7
  165.9 1.8 convolution_add_fusion.6
  167.7 0.7 convolution_add_fusion.5
  168.4 0.7 convolution_add_fusion.4
  169.2 0.7 convolution_add_fusion.3
  169.9 0.7 convolution_add_fusion.2
  170.7 0.7 convolution_add_fusion.1
  171.4 0.7 fusion.47
  172.7 18.0 %all_to_all.23 = f32[32,1,8]{2,1,0:T(1,128)S(1)} all-to-all(f32[32,1,8]{2,1,0:T(1,128)S(1)} %broadcast_in_dim.61), channel_id=1, replica_groups=mesh['rows'=32,'cols'=8] {'rows'}, dimensions={0} | all-to-all | bytes 2048 | tf_op jit(solution)/shard_map/all_to_all | solution.py:25
  191.2 0.3 add_convert_fusion
  191.6 1.8 broadcast_in_dim.62
  193.3 6.0 %all-to-all-start.2 = ((bf16[8,4,256,128]{3,2,1,0:T(8,128)(2,1)}), bf16[8,4,256,128]{3,2,1,0:T(8,128)(2,1)}, u32[]{:S(2)}, u32[]{:S(2)}) async-start(bf16[8,4,256,128]{3,2,1,0:T(8,128)(2,1)} %broadcast_in_dim.62), calls=%async_computation.2 | async-start | bytes 4194304 | tf_op jit(solution)/shard_map/all_to_all | solution.py:25
  199.4 26.3 %all-to-all-done.2 = bf16[8,4,256,128]{3,2,1,0:T(8,128)(2,1)} async-done(((bf16[8,4,256,128]{3,2,1,0:T(8,128)(2,1)}), bf16[8,4,256,128]{3,2,1,0:T(8,128)(2,1)}, u32[]{:S(2)}, u32[]{:S(2)}) %all-to-all-start.2) | async-done | bytes 2097184 | tf_op jit(solution)/shard_map/all_to_all | solution.py:25
  225.7 2.9 %copy.22 = bf16[4,256,8,128]{3,2,1,0:T(8,128)(2,1)S(1)} copy(bf16[4,256,8,128]{3,1,0,2:T(8,128)(2,1)} %bitcast.39) | data formatting | bytes 4194304 | tf_op jit(solution)/shard_map/transpose | solution.py:41
  228.7 2.4 fusion.52
  231.1 1.4 exponential_reduce_fusion
  232.5 0.7 broadcast_in_dim.64
  233.2 4.2 %all-to-all-start.3 = ((f32[8,3,1024]{2,1,0:T(4,128)}), f32[8,3,1024]{2,1,0:T(4,128)S(1)}, u32[]{:S(2)}, u32[]{:S(2)}) async-start(f32[8,3,1024]{2,1,0:T(4,128)} %broadcast_in_dim.64), calls=%async_computation.3 | async-start | bytes 262144 | tf_op jit(solution)/shard_map/all_to_all | solution.py:25
  237.4 5.3 %all-to-all-done.3 = f32[8,3,1024]{2,1,0:T(4,128)S(1)} async-done(((f32[8,3,1024]{2,1,0:T(4,128)}), f32[8,3,1024]{2,1,0:T(4,128)S(1)}, u32[]{:S(2)}, u32[]{:S(2)}) %all-to-all-start.3) | async-done | bytes 98336 | tf_op jit(solution)/shard_map/all_to_all | solution.py:25
  243.3 0.7 constant_dynamic-slice_fusion
  (93 shorter events, 2.9 us)
Async XLA Ops:
  7.2 221.5 %copy-start = (bf16[1024,1024]{1,0:T(8,128)(2,1)S(1)}, bf16[1024,1024]{1,0:T(8,128)(2,1)}, u32[]{:S(2)}) copy-start(bf16[1024,1024]{1,0:T(8,128)(2,1)} %param.23) | copy-start | bytes 6291460
  7.2 7.1 %copy-start.11 = (bf16[128]{0:T(256)(128)(2,1)S(1)}, bf16[128]{0:T(256)(128)(2,1)}, u32[]{:S(2)}) copy-start(bf16[128]{0:T(256)(128)(2,1)} %param.16) | copy-start | bytes 772
  7.2 56.1 %all-gather.3.cloned.1.call-start = ((), (), s32[]{:S(2)}) async-start(), calls=%async_computation.4 | async-start | bytes 3538944 | tf_op jit(solution)/shard_map/all_gather | solution.py:100
  14.6 5.7 %collective-permute-start = (bf16[1,256,128]{2,1,0:T(8,128)(2,1)S(1)}, bf16[1,256,128]{2,1,0:T(8,128)(2,1)S(1)}, u32[]{:S(2)}, u32[]{:S(2)}) collective-permute-start(bf16[1,256,128]{2,1,0:T(8,128)(2,1)S(1)} %get-tuple-element.32), channel_id=1, source_target_pairs={{0,8},{8,16},{16,24},{24,32},{32,40},{40,48},{48,56},{56,64},{64,7... | collective-permute-start | bytes 196616 | tf_op jit(solution)/shard_map/ppermute | solution.py:17
  19.0 5.2 %collective-permute-start.1 = (bf16[1,256,128]{2,1,0:T(8,128)(2,1)S(1)}, bf16[1,256,128]{2,1,0:T(8,128)(2,1)S(1)}, u32[]{:S(2)}, u32[]{:S(2)}) collective-permute-start(bf16[1,256,128]{2,1,0:T(8,128)(2,1)S(1)} %get-tuple-element.33), channel_id=1, source_target_pairs={{8,0},{16,8},{24,16},{32,24},{40,32},{48,40},{56,48},{64,56},{72,6... | collective-permute-start | bytes 196616 | tf_op jit(solution)/shard_map/ppermute | solution.py:18
  25.0 124.2 %all-gather.5.cloned.1.call-start = ((), (), s32[]{:S(2)}) async-start(), calls=%async_computation.5 | async-start | bytes 3538944 | tf_op jit(solution)/shard_map/all_gather | solution.py:100
  76.3 1.8 copy-start.5
  78.1 1.9 copy-start.3
  78.1 3.7 %copy-start.7 = (bf16[3,3,1024,128]{3,2,1,0:T(8,128)(2,1)S(1)}, bf16[3,3,1024,128]{3,2,1,0:T(8,128)(2,1)}, u32[]{:S(2)}) copy-start(bf16[3,3,1024,128]{3,2,1,0:T(8,128)(2,1)} %param.17) | copy-start | bytes 7077892
  79.9 1.8 copy-start.1
  85.5 19.8 %copy-start.12 = (f32[128]{0:T(128)S(1)}, f32[128]{0:T(128)}, u32[]{:S(2)}) copy-start(f32[128]{0:T(128)} %param.19) | copy-start | bytes 1540
  85.5 19.8 %copy-start.13 = (f32[128]{0:T(128)S(1)}, f32[128]{0:T(128)}, u32[]{:S(2)}) copy-start(f32[128]{0:T(128)} %param.18) | copy-start | bytes 1540
  105.5 3.7 %collective-permute-start.2 = (bf16[1,256,128]{2,1,0:T(8,128)(2,1)S(1)}, bf16[1,256,128]{2,1,0:T(8,128)(2,1)S(1)}, u32[]{:S(2)}, u32[]{:S(2)}) collective-permute-start(bf16[1,256,128]{2,1,0:T(8,128)(2,1)S(1)} %get-tuple-element.30), channel_id=1, source_target_pairs={{0,8},{8,16},{16,24},{24,32},{32,40},{40,48},{48,56},{56,64},{64,7... | collective-permute-start | bytes 196616 | tf_op jit(solution)/shard_map/ppermute | solution.py:17
  107.7 5.0 %collective-permute-start.3 = (bf16[1,256,128]{2,1,0:T(8,128)(2,1)S(1)}, bf16[1,256,128]{2,1,0:T(8,128)(2,1)S(1)}, u32[]{:S(2)}, u32[]{:S(2)}) collective-permute-start(bf16[1,256,128]{2,1,0:T(8,128)(2,1)S(1)} %get-tuple-element.31), channel_id=1, source_target_pairs={{8,0},{16,8},{24,16},{32,24},{40,32},{48,40},{56,48},{64,56},{72,6... | collective-permute-start | bytes 196616 | tf_op jit(solution)/shard_map/ppermute | solution.py:18
  162.2 1.8 copy-start.6
  164.0 1.9 copy-start.4
  164.0 3.7 %copy-start.8 = (bf16[3,3,1024,128]{3,2,1,0:T(8,128)(2,1)S(1)}, bf16[3,3,1024,128]{3,2,1,0:T(8,128)(2,1)}, u32[]{:S(2)}) copy-start(bf16[3,3,1024,128]{3,2,1,0:T(8,128)(2,1)} %param.20) | copy-start | bytes 7077892
  165.9 1.8 copy-start.2
  171.4 19.8 %copy-start.14 = (f32[128]{0:T(128)S(1)}, f32[128]{0:T(128)}, u32[]{:S(2)}) copy-start(f32[128]{0:T(128)} %param.22) | copy-start | bytes 1540
  171.4 19.8 %copy-start.15 = (f32[128]{0:T(128)S(1)}, f32[128]{0:T(128)}, u32[]{:S(2)}) copy-start(f32[128]{0:T(128)} %param.21) | copy-start | bytes 1540
  191.5 1.8 copy-start.9
  193.3 6.0 %copy-start.10 = (s32[4,256]{1,0:T(4,128)S(1)}, s32[4,256]{1,0:T(4,128)}, u32[]{:S(2)}) copy-start(s32[4,256]{1,0:T(4,128)} %param.12) | copy-start | bytes 12292
  193.3 32.4 %all-to-all-start.2 = ((bf16[8,4,256,128]{3,2,1,0:T(8,128)(2,1)}), bf16[8,4,256,128]{3,2,1,0:T(8,128)(2,1)}, u32[]{:S(2)}, u32[]{:S(2)}) async-start(bf16[8,4,256,128]{3,2,1,0:T(8,128)(2,1)} %broadcast_in_dim.62), calls=%async_computation.2 | async-start | bytes 4194304 | tf_op jit(solution)/shard_map/all_to_all | solution.py:25
  233.2 9.5 %all-to-all-start.3 = ((f32[8,3,1024]{2,1,0:T(4,128)}), f32[8,3,1024]{2,1,0:T(4,128)S(1)}, u32[]{:S(2)}, u32[]{:S(2)}) async-start(f32[8,3,1024]{2,1,0:T(4,128)} %broadcast_in_dim.64), calls=%async_computation.3 | async-start | bytes 262144 | tf_op jit(solution)/shard_map/all_to_all | solution.py:25
Sparse Core Ops, SparseCore 0:
  25.1 38.1 all-gather.2
  113.7 35.5 all-gather.4
where the time goes:
time: 251 us
  waiting for transfers between devices  113 us (45%)
  local copies, waits for them, and re-layouts  38.3 us (15%)
  blocking collectives  36.1 us (14%)
  matrix products  22.1 us (9%)
  starting transfers between devices  19.7 us (8%)
  between operations  14.6 us (6%)
  other arithmetic  7.12 us (3%)
    all_gather x2, waiting for transfers between devices, convolve(): lax.all_gather(rimmed, 'cols', axis=2, tiled=True)  73.9 us
    all_to_all x2, blocking collectives, sent_to_all(): return lax.all_to_all(copies, axis, split_axis=0, concat_axis=0, tiled=True)  36.1 us
    all_to_all x2, waiting for transfers between devices, sent_to_all(): return lax.all_to_all(copies, axis, split_axis=0, concat_axis=0, tiled=True)  31.6 us
    slice x2, local copies, waits for them, and re-layouts, add_taps(): padded[shift_row:shift_row + rows_here, shift_col:shift_col + width]  26 us
    dot_general x18, matrix products, add_taps(): total = total + jnp.dot(window, taps, preferred_element_type=jnp.float32)  19.7 us
    all_to_all x2, starting transfers between devices, sent_to_all(): return lax.all_to_all(copies, axis, split_axis=0, concat_axis=0, tiled=True)  10.3 us
    ppermute x2, waiting for transfers between devices, with_halo(): after = lax.ppermute(leading, axis, down)  7.41 us
    ppermute x2, starting transfers between devices, with_halo(): before = lax.ppermute(last, axis, up)  6.61 us
  transfers between devices with their start and end apart: 8, of which 6 were waited for; matrix products, arithmetic and copies ran while one was open for 0% of the time, Pallas kernels for 0%

commit v1 on v0

v1 whole, which is shorter than its diff:
```python
import functools

import jax
import jax.numpy as jnp
from jax import lax
from jax.experimental import pallas as pl
from jax.experimental.pallas import tpu as pltpu
from jax.sharding import PartitionSpec as P

GROUP_WIDTH = 32
MESH = pl.DeviceIdType.MESH
F32 = jnp.float32
BF16 = jnp.bfloat16
XP, XM, OWN, FROM_P, FROM_M, FAR, FWD, UP, DOWN, UPF, DOWNF = range(11)


def group_sum(row):
    width = row.shape[1]
    a = lax.broadcasted_iota(jnp.int32, (width, width), 0) // GROUP_WIDTH
    b = lax.broadcasted_iota(jnp.int32, (width, width), 1) // GROUP_WIDTH
    ones = jnp.where(a == b, 1.0, 0.0).astype(F32)
    rows = jnp.broadcast_to(row, (8, width))
    return jnp.dot(
        rows, ones, preferred_element_type=F32, precision=lax.Precision.HIGHEST
    )[0:1]


def kernel(
    num_rows,
    num_cols,
    ids_ref,
    keep_ref,
    order_ref,
    table_hbm,
    mask_ref,
    conv_one_hbm,
    gain_one_ref,
    bias_one_ref,
    conv_two_hbm,
    gain_two_ref,
    bias_two_ref,
    head_hbm,
    features_ref,
    logp_ref,
    table_ref,
    wide_ref,
    conv_one_ref,
    conv_two_ref,
    head_ref,
    ids_vmem,
    ids_smem,
    tokens_ref,
    looked_ref,
    field_one,
    field_two,
    field_three,
    total_ref,
    conv_ref,
    stat_send,
    stat_all,
    logits_ref,
    last_send,
    last_all,
    load_sems,
    send_sems,
    recv_sems,
    stat_send_sems,
    stat_recv_sems,
    last_send_sems,
    last_recv_sems,
):
    height, width = ids_ref.shape
    vocab = table_hbm.shape[0]
    lanes = table_hbm.shape[1]
    channels = num_cols * lanes
    r = lax.axis_index("rows")
    k = lax.axis_index("cols")
    chips = num_cols // 2
    core = lax.rem(k, 2)
    chip = k // 2
    partner = k + 1 - 2 * core

    def piece(step, c):
        return lax.rem(chip + step, chips) * 2 + c

    right, left = piece(1, core), piece(chips - 1, core)
    above = lax.rem(r + num_rows - 1, num_rows)
    below = lax.rem(r + 1, num_rows)

    loads = [
        pltpu.make_async_copy(src, dst, load_sems.at[n])
        for n, (src, dst) in enumerate(
            (
                (table_hbm, table_ref),
                (conv_one_hbm, conv_one_ref),
                (conv_two_hbm, conv_two_ref),
                (head_hbm, head_ref),
            )
        )
    ]
    for load in loads:
        load.start()

    barrier = pltpu.get_barrier_semaphore()

    def greet_row(d, _):
        pl.semaphore_signal(
            barrier,
            inc=1,
            device_id={"rows": lax.rem(r + d, num_rows)},
            device_id_type=MESH,
        )
        return 0

    def greet_col(d, _):
        pl.semaphore_signal(
            barrier,
            inc=1,
            device_id={"cols": lax.rem(k + d, num_cols)},
            device_id_type=MESH,
        )
        return 0

    lax.fori_loop(1, num_rows, greet_row, 0)
    lax.fori_loop(1, num_cols, greet_col, 0)

    half = height * width * num_rows // 2
    parts = width // 128
    for i in range(height):
        for j in range(parts):
            at = (slice(i, i + 1), slice(128 * j, 128 * j + 128))
            n = i * parts + j
            visible = (keep_ref[at] == 1) | (order_ref[n : n + 1, :] >= half)
            ids_vmem[n : n + 1, :] = jnp.where(visible, ids_ref[at], vocab)
    to_smem = pltpu.make_async_copy(ids_vmem, ids_smem, load_sems.at[4])
    to_smem.start()
    for i in range(height):
        row = ids_ref[i : i + 1, :].astype(F32)
        tokens_ref[i] = jnp.broadcast_to(row, (128, width)).T
    loads[0].wait()
    step_rows = 512

    def widen(n, _):
        at = pl.ds(pl.multiple_of(n * step_rows, step_rows), step_rows)
        wide_ref[at, :] = table_ref[at, :].astype(F32)
        return 0

    lax.fori_loop(0, vocab // step_rows, widen, 0)
    wide_ref[vocab : vocab + 8, :] = jnp.broadcast_to(mask_ref[...].astype(F32), (8, lanes))
    to_smem.wait()

    pl.semaphore_wait(barrier, num_rows - 1 + num_cols - 1)

    pending = []

    class Gather:
        def __init__(self, n, field, halo):
            self.n, self.field, self.halo = n, field, halo
            self.off = 1 if halo else 0

        def copy(self, kind, slot, owner, row, device, to_row=None):
            to_row = row if to_row is None else to_row
            return pltpu.make_async_remote_copy(
                src_ref=self.field.at[owner, row],
                dst_ref=self.field.at[owner, to_row],
                send_sem=send_sems.at[self.n, kind, slot],
                recv_sem=recv_sems.at[self.n, kind, slot],
                device_id=device,
                device_id_type=MESH,
            )

        def send(self, *args, **kw):
            c = self.copy(*args, **kw)
            c.start()
            pending.append(c)

        def wait(self, kind, slot, owner, row):
            self.copy(kind, slot, owner, row, {"cols": partner}).wait_recv()

        def halo_out(self, q, owner, i):
            if not self.halo:
                return
            if i == 0:
                self.send(UP, q, owner, 1, {"rows": above}, to_row=height + 1)
            if i == height - 1:
                self.send(DOWN, q, owner, height, {"rows": below}, to_row=0)

        def own(self, i):
            row = i + self.off
            self.send(XP, i, k, row, {"cols": right})
            self.send(XM, i, k, row, {"cols": left})
            self.halo_out(0, k, i)
            self.send(OWN, i, k, row, {"cols": partner})

        def from_left(self, i):
            row, owner = i + self.off, left
            self.wait(XP, i, owner, row)
            if i in (0, 1):
                self.send(FWD, i, owner, row, {"cols": right})
            self.halo_out(1, owner, i)
            self.send(FROM_P, i, owner, row, {"cols": partner})

        def from_right(self, i):
            row, owner = i + self.off, right
            self.wait(XM, i, owner, row)
            if i in (2, 3):
                self.send(FWD, i, owner, row, {"cols": left})
            self.halo_out(2, owner, i)
            self.send(FROM_M, i, owner, row, {"cols": partner})

        def from_far(self, i):
            row, owner = i + self.off, piece(2, core)
            self.wait(FWD, i, owner, row)
            self.halo_out(3, owner, i)
            self.send(FAR, i, owner, row, {"cols": partner})

        def owner_of(self, q, c):
            return piece((0, chips - 1, 1, 2)[q], c)

        def halo_in(self, q):
            owner = self.owner_of(q, core)
            self.wait(UP, q, owner, height + 1)
            self.send(UPF, q, owner, height + 1, {"cols": partner})
            self.wait(DOWN, q, owner, 0)
            self.send(DOWNF, q, owner, 0, {"cols": partner})

        def rest(self, q):
            owner = self.owner_of(q, 1 - core)
            for i in range(height):
                self.wait((OWN, FROM_P, FROM_M, FAR)[q], i, owner, i + self.off)
            if self.halo:
                self.wait(UPF, q, owner, height + 1)
                self.wait(DOWNF, q, owner, 0)

    def convolve(gather, weight_ref, q):
        field = gather.field
        at = lax.rem(chip + (0, chips - 1, 1, 2)[q], chips)
        one, two = at * 2, at * 2 + 1
        rows = pl.ds(pl.multiple_of(at * 2 * lanes, 2 * lanes), 2 * lanes)
        weights = jnp.concatenate(
            [
                jnp.concatenate([weight_ref[a, b, rows, :] for b in range(3)], axis=1)
                for a in range(3)
            ],
            axis=0,
        )
        tall = 2

        def block(n, _):
            first = n * tall
            keep_up = jnp.logical_or(r > 0, n > 0)
            keep_down = jnp.logical_or(r < num_rows - 1, n < height // tall - 1)
            columns = []
            for a in range(3):
                for p in (one, two):
                    tiles = [field[p, first + a + t] for t in range(tall)]
                    if a == 0:
                        tiles[0] = jnp.where(keep_up, tiles[0], jnp.zeros_like(tiles[0]))
                    if a == 2:
                        tiles[-1] = jnp.where(keep_down, tiles[-1], jnp.zeros_like(tiles[-1]))
                    columns.append(jnp.concatenate(tiles, axis=0))
            product = jnp.dot(
                jnp.concatenate(columns, axis=1), weights, preferred_element_type=F32
            )
            at_rows = pl.ds(pl.multiple_of(first * width, tall * width), tall * width)
            if q == 0:
                total_ref[at_rows, :] = product
            else:
                total_ref[at_rows, :] += product
            return 0

        lax.fori_loop(0, height // tall, block, 0)

    def shifted_sum():
        index = lax.broadcasted_iota(jnp.int32, (width, lanes), 0)
        for i in range(height):
            at = slice(i * width, (i + 1) * width)
            before = pltpu.roll(total_ref[at, 0:lanes], 1, axis=0)
            after = pltpu.roll(total_ref[at, 2 * lanes : 3 * lanes], width - 1, axis=0)
            conv_ref[at, :] = (
                jnp.where(index == 0, 0.0, before)
                + total_ref[at, lanes : 2 * lanes]
                + jnp.where(index == width - 1, 0.0, after)
            )

    def statistics(n):
        count = height * width * GROUP_WIDTH
        values = conv_ref[...]
        mean = group_sum(jnp.sum(values, axis=0, keepdims=True)) / count
        deviation = values - mean
        square = group_sum(jnp.sum(deviation * deviation, axis=0, keepdims=True))
        both = jnp.concatenate([mean, square], axis=0)
        stat_send[n] = both

        def tell(d, _):
            to = lax.rem(r + d, num_rows)
            pltpu.make_async_remote_copy(
                src_ref=stat_send.at[n],
                dst_ref=stat_all.at[n, d],
                send_sem=stat_send_sems.at[n],
                recv_sem=stat_recv_sems.at[n],
                device_id={"rows": to},
                device_id_type=MESH,
            ).start()
            return 0

        lax.fori_loop(1, num_rows, tell, 0)
        stat_all[n, 0] = both
        everything = stat_all.at[n, pl.ds(1, num_rows - 1)]
        arrived = pltpu.make_async_remote_copy(
            src_ref=everything,
            dst_ref=everything,
            send_sem=stat_send_sems.at[n],
            recv_sem=stat_recv_sems.at[n],
            device_id={"rows": above},
            device_id_type=MESH,
        )
        arrived.wait_recv()
        pending.append(arrived)
        stats = stat_all[n]
        means = stats[:, 0, :]
        mean = jnp.sum(means, axis=0, keepdims=True) / num_rows
        spread = means - mean
        square = jnp.sum(stats[:, 1, :], axis=0, keepdims=True)
        square = square + count * jnp.sum(spread * spread, axis=0, keepdims=True)
        return mean, square / (count * num_rows)

    first = Gather(0, field_one, True)

    def look_up(i):
        unroll = 16

        def some(n, _):
            base = n * unroll
            line = i * parts + base // 128
            lane = lax.rem(base, 128)
            for u in range(unroll):
                row = ids_smem[line, lane + u]
                looked_ref[pl.ds(base + u, 1), :] = wide_ref[pl.ds(row, 1), :]
            return 0

        lax.fori_loop(0, width // unroll, some, 0)
        first.field[k, i + 1] = looked_ref[...].astype(BF16)

    def run_gather(gather, make, early):
        make(0)
        gather.own(0)
        make(3)
        gather.own(3)
        make(1)
        gather.own(1)
        gather.from_left(0)
        gather.from_right(3)
        make(2)
        gather.own(2)
        gather.from_right(0)
        gather.from_left(3)
        if gather.halo:
            gather.halo_in(0)
        gather.rest(0)
        early()
        gather.from_left(1)
        gather.from_right(2)
        if gather.halo:
            gather.halo_in(1)
            gather.halo_in(2)
        gather.from_right(1)
        gather.from_left(2)
        gather.from_far(0)
        gather.from_far(3)

    def conv_layer(gather, make, load, weight_ref, n):
        def early():
            load.wait()
            convolve(gather, weight_ref, 0)

        run_gather(gather, make, early)
        gather.rest(1)
        convolve(gather, weight_ref, 1)
        gather.from_far(1)
        gather.from_far(2)
        gather.halo_in(3)
        gather.rest(2)
        convolve(gather, weight_ref, 2)
        gather.rest(3)
        convolve(gather, weight_ref, 3)
        shifted_sum()
        return statistics(n)

    mean, variance = conv_layer(first, look_up, loads[1], conv_one_ref, 0)

    second = Gather(1, field_two, True)
    root_one = jnp.sqrt(variance + 1e-5)
    gain_one = gain_one_ref[...]
    bias_one = bias_one_ref[...]

    def make_hidden(i):
        at = slice(i * width, (i + 1) * width)
        v = (conv_ref[at, :] - mean) / root_one * gain_one + bias_one
        second.field[k, i + 1] = (v / (1.0 + jnp.exp(-v))).astype(BF16)

    mean_two, variance_two = conv_layer(second, make_hidden, loads[2], conv_two_ref, 1)

    third = Gather(2, field_three, False)
    root_two = jnp.sqrt(variance_two + 1e-5)
    gain_two = gain_two_ref[...]
    bias_two = bias_two_ref[...]

    def make_features(i):
        at = slice(i * width, (i + 1) * width)
        v = (conv_ref[at, :] - mean_two) / root_two * gain_two + bias_two
        out = (first.field[k, i + 1].astype(F32) + v).astype(BF16)
        third.field[k, i] = out
        features_ref[i] = out

    vocab_here = head_hbm.shape[1]
    tiles = vocab_here // 128

    def head_row(i):
        left_side = jnp.concatenate([third.field[p, i] for p in range(num_cols)], axis=1)
        logits_ref[...] = jnp.dot(left_side, head_ref[...], preferred_element_type=F32)
        most = logits_ref[:, 0:128]
        for t in range(1, tiles):
            most = jnp.maximum(most, logits_ref[:, 128 * t : 128 * t + 128])
        top = jnp.max(most, axis=1, keepdims=True)
        token = tokens_ref[i]
        lane = lax.broadcasted_iota(jnp.int32, (width, 128), 1)
        summed = jnp.zeros((width, 128), F32)
        picked = jnp.zeros((width, 128), F32)
        for t in range(tiles):
            part = logits_ref[:, 128 * t : 128 * t + 128]
            summed = summed + jnp.exp(part - top)
            ids = (lane + (k * vocab_here + 128 * t)).astype(F32)
            picked = picked + jnp.where(ids == token, part, 0.0)
        top_row = jnp.max(most.T, axis=0, keepdims=True)
        sum_row = jnp.sum(summed.T, axis=0, keepdims=True)
        pick_row = jnp.sum(picked.T, axis=0, keepdims=True)
        for s, row in enumerate((top_row, sum_row, pick_row)):
            for b in range(parts):
                last_send[b, s, pl.ds(i, 1), :] = row[:, 128 * b : 128 * b + 128]

    def head_rows(start, step):
        def one(n, _):
            head_row(start + step * n)
            return 0

        lax.fori_loop(0, 2, one, 0)

    run_gather(third, make_features, lambda: None)
    for q in range(1, 4):
        for i in (0, 3):
            third.wait((OWN, FROM_P, FROM_M, FAR)[q], i, third.owner_of(q, 1 - core), i)
    loads[3].wait()
    head_rows(0, 3)
    third.from_far(1)
    third.from_far(2)
    for q in range(1, 4):
        for i in (1, 2):
            third.wait((OWN, FROM_P, FROM_M, FAR)[q], i, third.owner_of(q, 1 - core), i)
    head_rows(1, 1)

    per_block = num_cols // parts

    def exchange(d):
        to = lax.rem(k + d, num_cols)
        return pltpu.make_async_remote_copy(
            src_ref=last_send.at[to // per_block],
            dst_ref=last_all.at[d],
            send_sem=last_send_sems.at[d],
            recv_sem=last_recv_sems.at[d],
            device_id={"cols": to},
            device_id_type=MESH,
        )

    for d in range(1, num_cols):
        exchange(d).start()
    last_all[0] = last_send[k // per_block]
    for d in range(1, num_cols):
        exchange(d).wait_recv()
    top = last_all[0, 0]
    for d in range(1, num_cols):
        top = jnp.maximum(top, last_all[d, 0])
    summed = jnp.zeros_like(top)
    picked = jnp.zeros_like(top)
    for d in range(num_cols):
        summed = summed + last_all[d, 1] * jnp.exp(last_all[d, 0] - top)
        picked = picked + last_all[d, 2]
    logp = picked - top - jnp.log(summed)
    mine = width // num_cols
    place = lax.rem(k, per_block)
    out = logp[:, 0:mine]
    for b in range(1, per_block):
        out = jnp.where(place == b, logp[:, mine * b : mine * b + mine], out)
    logp_ref[...] = out

    for copy in pending:
        copy.wait_send()
    for d in range(1, num_cols):
        exchange(d).wait_send()


def local(
    token_ids,
    keep_mask,
    remask_order,
    embed_table,
    mask_embed,
    conv_one,
    gain_one,
    bias_one,
    conv_two,
    gain_two,
    bias_two,
    head_weight,
):
    num_rows, num_cols = lax.axis_size("rows"), lax.axis_size("cols")
    height, width = token_ids.shape
    vocab, lanes = embed_table.shape
    lines = height * width // 128
    in_vmem = pl.BlockSpec(memory_space=pltpu.VMEM)
    anywhere = pl.BlockSpec(memory_space=pl.ANY)
    return pl.pallas_call(
        functools.partial(kernel, num_rows, num_cols),
        name="denoise",
        out_shape=(
            jax.ShapeDtypeStruct((height, width, lanes), BF16),
            jax.ShapeDtypeStruct((height, width // num_cols), F32),
        ),
        in_specs=[
            in_vmem,
            in_vmem,
            in_vmem,
            anywhere,
            in_vmem,
            anywhere,
            in_vmem,
            in_vmem,
            anywhere,
            in_vmem,
            in_vmem,
            anywhere,
        ],
        out_specs=(in_vmem, in_vmem),
        scratch_shapes=[
            pltpu.VMEM((vocab, lanes), BF16),
            pltpu.VMEM((vocab + 8, lanes), F32),
            pltpu.VMEM(conv_one.shape, BF16),
            pltpu.VMEM(conv_two.shape, BF16),
            pltpu.VMEM(head_weight.shape, BF16),
            pltpu.VMEM((lines, 128), jnp.int32),
            pltpu.SMEM((lines, 128), jnp.int32),
            pltpu.VMEM((height, width, 128), F32),
            pltpu.VMEM((width, lanes), F32),
            pltpu.VMEM((num_cols, height + 2, width, lanes), BF16),
            pltpu.VMEM((num_cols, height + 2, width, lanes), BF16),
            pltpu.VMEM((num_cols, height, width, lanes), BF16),
            pltpu.VMEM((height * width, 3 * lanes), F32),
            pltpu.VMEM((height * width, lanes), F32),
            pltpu.VMEM((2, 2, lanes), F32),
            pltpu.VMEM((2, num_rows, 2, lanes), F32),
            pltpu.VMEM((width, head_weight.shape[1]), F32),
            pltpu.VMEM((width // 128, 3, height, 128), F32),
            pltpu.VMEM((num_cols, 3, height, 128), F32),
            pltpu.SemaphoreType.DMA((5,)),
            pltpu.SemaphoreType.DMA((3, 11, 4)),
            pltpu.SemaphoreType.DMA((3, 11, 4)),
            pltpu.SemaphoreType.DMA((2,)),
            pltpu.SemaphoreType.DMA((2,)),
            pltpu.SemaphoreType.DMA((num_cols,)),
            pltpu.SemaphoreType.DMA((num_cols,)),
        ],
        compiler_params=pltpu.CompilerParams(
            collective_id=0, has_side_effects=True, vmem_limit_bytes=60 * 1024 * 1024
        ),
    )(
        token_ids,
        keep_mask,
        remask_order.reshape(lines, 128),
        embed_table,
        mask_embed.reshape(1, lanes),
        conv_one,
        gain_one.reshape(1, lanes),
        bias_one.reshape(1, lanes),
        conv_two,
        gain_two.reshape(1, lanes),
        bias_two.reshape(1, lanes),
        head_weight,
    )


def solution(mesh):
    in_specs = (
        P("rows", None),
        P("rows", None),
        P("rows"),
        P(None, "cols"),
        P("cols"),
        P(None, None, None, "cols"),
        P("cols"),
        P("cols"),
        P(None, None, None, "cols"),
        P("cols"),
        P("cols"),
        P(None, "cols"),
    )
    out_specs = (P("rows", None, "cols"), P("rows", "cols"))
    return jax.shard_map(local, mesh=mesh, in_specs=in_specs, out_specs=out_specs, check_vma=False)
```

time: 251 us -> 88.8 us (0.35)
  waiting for transfers between devices: 113 us -> 0 us
  Pallas kernels: 0 us -> 85 us
  blocking collectives: 36.1 us -> 0 us
  local copies, waits for them, and re-layouts: 38.3 us -> 2.92 us
  matrix products: 22.1 us -> 0 us
  starting transfers between devices: 19.7 us -> 0 us
  between operations: 14.6 us -> 0.64 us
  other arithmetic: 7.12 us -> 0 us
    pallas_call x0 -> x1, Pallas kernels: none -> 85 us  [local(): pl.pallas_call(functools.partial(kernel, num_rows, num_cols), name='denoi...]
    all_gather x2 -> x0, waiting for transfers between devices: 73.9 us -> none  [convolve(): lax.all_gather(rimmed, 'cols', axis=2, tiled=True)]
    all_to_all x2 -> x0, blocking collectives: 36.1 us -> none  [sent_to_all(): return lax.all_to_all(copies, axis, split_axis=0, concat_axis=0, tiled=True)]
    all_to_all x2 -> x0, waiting for transfers between devices: 31.6 us -> none  [sent_to_all(): return lax.all_to_all(copies, axis, split_axis=0, concat_axis=0, tiled=True)]
    slice x17 -> x0, local copies, waits for them, and re-layouts: 26.4 us -> none  [the longest x2 26 us: add_taps(): padded[shift_row:shift_row + rows_here, shift_col:shift_col + width]]
    dot_general x19 -> x0, matrix products: 22.1 us -> none  [the longest x18 19.7 us: add_taps(): total = total + jnp.dot(window, taps, preferred_element_type=jnp.float32)]
    all_to_all x2 -> x0, starting transfers between devices: 10.3 us -> none  [sent_to_all(): return lax.all_to_all(copies, axis, split_axis=0, concat_axis=0, tiled=True)]
    ppermute x4 -> x0, starting transfers between devices: 9.37 us -> none  [the longest x2 6.61 us: with_halo(): before = lax.ppermute(last, axis, up)]
  transfers between devices with their start and end apart: 8 -> 0, of which waited for: 6 -> 0; matrix products, arithmetic and copies ran while one was open for 0% -> 0% of each run, Pallas kernels for 0% -> 0%
where the time goes in v1:
time: 88.8 us; the launch traced here: 88.6 us
  Pallas kernels  85 us (96%)
  local copies, waits for them, and re-layouts  2.92 us (3%)
    pallas_call x1, Pallas kernels, local(): pl.pallas_call(functools.partial(kernel, num_rows, num_cols), name='denoi...  85 us
    unnamed x2, local copies, waits for them, and re-layouts  2.92 us

profile of v1, /device:TPU:1, one launch (start us, length us, event | category | flops | bytes accessed | tf_op | source)
XLA Modules:
  0.0 88.6 jit_solution(15570864563341310759)
XLA Ops:
  0.6 85.0 %denoise.1 = (bf16[4,256,128]{2,1,0:T(8,128)(2,1)}, f32[4,32]{1,0:T(4,128)}) custom-call(s32[4,256]{1,0:T(4,128)} %ids_ref.1, s32[4,256]{1,0:T(4,128)} %keep_ref.1, s32[8,128]{1,0:T(8,128)} %bitcast.6, bf16[8192,128]{1,0:T(8,128)(2,1)} %table_hbm.1, bf16[1,128]{1,0:T(2,128)(2,1)} %bitcast.7, bf16[3,3,1024,128]{3,2,1,0:T(8,128)(2,1)} %conv_one_hbm.1, ...), custom_call_target="tpu_custom_call" | custom-call | tf_op jit(solution)/shard_map/denoise/pallas_call | solution.py:522
  85.7 1.7 %copy.16 = bf16[4,256,128]{2,1,0:T(8,128)(2,1)} copy(bf16[4,256,128]{2,1,0:T(8,128)(2,1)} %get-tuple-element.4) | data formatting | bytes 524288
  87.3 1.2 %copy.17 = f32[4,32]{1,0:T(4,128)} copy(f32[4,32]{1,0:T(4,128)} %get-tuple-element.5) | data formatting | bytes 1024

commit v2 on v1

--- a/solution.py
+++ b/solution.py
@@ -58,6 +58,9 @@
     conv_ref,
     stat_send,
     stat_all,
+    coef_send,
+    coef_all,
+    hidden_ref,
     logits_ref,
     last_send,
     last_all,
@@ -66,6 +69,8 @@
     recv_sems,
     stat_send_sems,
     stat_recv_sems,
+    coef_send_sems,
+    coef_recv_sems,
     last_send_sems,
     last_recv_sems,
 ):
@@ -149,8 +154,6 @@
     wide_ref[vocab : vocab + 8, :] = jnp.broadcast_to(mask_ref[...].astype(F32), (8, lanes))
     to_smem.wait()
 
-    pl.semaphore_wait(barrier, num_rows - 1 + num_cols - 1)
-
     pending = []
 
     class Gather:
@@ -187,10 +190,14 @@
 
         def own(self, i):
             row = i + self.off
-            self.send(XP, i, k, row, {"cols": right})
-            self.send(XM, i, k, row, {"cols": left})
             self.halo_out(0, k, i)
             self.send(OWN, i, k, row, {"cols": partner})
+
+        def own_right(self, i):
+            self.send(XP, i, k, i + self.off, {"cols": right})
+
+        def own_left(self, i):
+            self.send(XM, i, k, i + self.off, {"cols": left})
 
         def from_left(self, i):
             row, owner = i + self.off, left
@@ -232,9 +239,27 @@
                 self.wait(UPF, q, owner, height + 1)
                 self.wait(DOWNF, q, owner, 0)
 
-    def convolve(gather, weight_ref, q):
-        field = gather.field
-        at = lax.rem(chip + (0, chips - 1, 1, 2)[q], chips)
+    def at_chip(q):
+        return lax.rem(chip + (0, chips - 1, 1, 2)[q], chips)
+
+    def normalise(gather, q, slots):
+        for c in range(2):
+            owner = at_chip(q) * 2 + c
+            d = lax.rem(k - owner + num_cols, num_cols)
+            scale = coef_all[0, d, 0:1, :]
+            for slot in slots:
+                which = 1 + jnp.where(slot > 0, 1, 0) + jnp.where(slot > height, 1, 0)
+                shift = coef_all[0, d, pl.ds(which, 1), :]
+                inside = jnp.logical_and(
+                    jnp.logical_or(r > 0, slot > 0),
+                    jnp.logical_or(r < num_rows - 1, slot <= height),
+                )
+                v = gather.field[owner, slot].astype(F32) * (0.5 * scale) + 0.5 * shift
+                v = v + v * jnp.tanh(v)
+                hidden_ref[owner, slot] = jnp.where(inside, v, 0.0).astype(BF16)
+
+    def convolve(field, masked, weight_ref, q, beside=None):
+        at = at_chip(q)
         one, two = at * 2, at * 2 + 1
         rows = pl.ds(pl.multiple_of(at * 2 * lanes, 2 * lanes), 2 * lanes)
         weights = jnp.concatenate(
@@ -254,9 +279,9 @@
             for a in range(3):
                 for p in (one, two):
                     tiles = [field[p, first + a + t] for t in range(tall)]
-                    if a == 0:
+                    if masked and a == 0:
                         tiles[0] = jnp.where(keep_up, tiles[0], jnp.zeros_like(tiles[0]))
-                    if a == 2:
+                    if masked and a == 2:
                         tiles[-1] = jnp.where(keep_down, tiles[-1], jnp.zeros_like(tiles[-1]))
                     columns.append(jnp.concatenate(tiles, axis=0))
             product = jnp.dot(
@@ -267,63 +292,108 @@
                 total_ref[at_rows, :] = product
             else:
                 total_ref[at_rows, :] += product
+            if beside is not None:
+                beside(n)
             return 0
 
         lax.fori_loop(0, height // tall, block, 0)
 
-    def shifted_sum():
+    def shifted_row(i):
         index = lax.broadcasted_iota(jnp.int32, (width, lanes), 0)
-        for i in range(height):
-            at = slice(i * width, (i + 1) * width)
-            before = pltpu.roll(total_ref[at, 0:lanes], 1, axis=0)
-            after = pltpu.roll(total_ref[at, 2 * lanes : 3 * lanes], width - 1, axis=0)
-            conv_ref[at, :] = (
-                jnp.where(index == 0, 0.0, before)
-                + total_ref[at, lanes : 2 * lanes]
-                + jnp.where(index == width - 1, 0.0, after)
+        at = slice(i * width, (i + 1) * width)
+        before = pltpu.roll(total_ref[at, 0:lanes], 1, axis=0)
+        after = pltpu.roll(total_ref[at, 2 * lanes : 3 * lanes], width - 1, axis=0)
+        return (
+            jnp.where(index == 0, 0.0, before)
+            + total_ref[at, lanes : 2 * lanes]
+            + jnp.where(index == width - 1, 0.0, after)
+        )
+
+    positions = height * width
+    count = positions * GROUP_WIDTH
+
+    class Norm:
+        def __init__(self, n, gain, bias):
+            self.n, self.gain, self.bias = n, gain, bias
+            self.centre = self.sums = self.squares = None
+
+        def row(self, i, gather):
+            values = shifted_row(i)
+            if self.centre is None:
+                self.centre = jnp.sum(values, axis=0, keepdims=True) / width
+            values = values - self.centre
+            gather.field[k, i + gather.off] = values.astype(BF16)
+            conv_ref[i * width : (i + 1) * width, :] = values
+            total = jnp.sum(values, axis=0, keepdims=True)
+            square = jnp.sum(values * values, axis=0, keepdims=True)
+            self.sums = total if self.sums is None else self.sums + total
+            self.squares = square if self.squares is None else self.squares + square
+
+        def tell(self):
+            n = self.n
+            mean = group_sum(self.sums + positions * self.centre) / count
+            off = self.centre - mean
+            square = group_sum(self.squares + 2 * off * self.sums + positions * off * off)
+            both = jnp.concatenate([mean, square, self.centre, self.centre], axis=0)
+            stat_send[n] = both
+            stat_all[n, 0] = both
+
+            def one(d, _):
+                pltpu.make_async_remote_copy(
+                    src_ref=stat_send.at[n],
+                    dst_ref=stat_all.at[n, d],
+                    send_sem=stat_send_sems.at[n],
+                    recv_sem=stat_recv_sems.at[n],
+                    device_id={"rows": lax.rem(r + d, num_rows)},
+                    device_id_type=MESH,
+                ).start()
+                return 0
+
+            lax.fori_loop(1, num_rows, one, 0)
+
+        def coef(self, d):
+            n = self.n
+            return pltpu.make_async_remote_copy(
+                src_ref=coef_send.at[n],
+                dst_ref=coef_all.at[n, d],
+                send_sem=coef_send_sems.at[n, d],
+                recv_sem=coef_recv_sems.at[n, d],
+                device_id={"cols": lax.rem(k + d, num_cols)},
+                device_id_type=MESH,
             )
 
-    def statistics(n):
-        count = height * width * GROUP_WIDTH
-        values = conv_ref[...]
-        mean = group_sum(jnp.sum(values, axis=0, keepdims=True)) / count
-        deviation = values - mean
-        square = group_sum(jnp.sum(deviation * deviation, axis=0, keepdims=True))
-        both = jnp.concatenate([mean, square], axis=0)
-        stat_send[n] = both
-
-        def tell(d, _):
-            to = lax.rem(r + d, num_rows)
-            pltpu.make_async_remote_copy(
-                src_ref=stat_send.at[n],
-                dst_ref=stat_all.at[n, d],
+        def settle(self):
+            n = self.n
+            everything = stat_all.at[n, pl.ds(1, num_rows - 1)]
+            arrived = pltpu.make_async_remote_copy(
+                src_ref=everything,
+                dst_ref=everything,
                 send_sem=stat_send_sems.at[n],
                 recv_sem=stat_recv_sems.at[n],
-                device_id={"rows": to},
+                device_id={"rows": above},
                 device_id_type=MESH,
-            ).start()
-            return 0
-
-        lax.fori_loop(1, num_rows, tell, 0)
-        stat_all[n, 0] = both
-        everything = stat_all.at[n, pl.ds(1, num_rows - 1)]
-        arrived = pltpu.make_async_remote_copy(
-            src_ref=everything,
-            dst_ref=everything,
-            send_sem=stat_send_sems.at[n],
-            recv_sem=stat_recv_sems.at[n],
-            device_id={"rows": above},
-            device_id_type=MESH,
-        )
-        arrived.wait_recv()
-        pending.append(arrived)
-        stats = stat_all[n]
-        means = stats[:, 0, :]
-        mean = jnp.sum(means, axis=0, keepdims=True) / num_rows
-        spread = means - mean
-        square = jnp.sum(stats[:, 1, :], axis=0, keepdims=True)
-        square = square + count * jnp.sum(spread * spread, axis=0, keepdims=True)
-        return mean, square / (count * num_rows)
+            )
+            arrived.wait_recv()
+            pending.append(arrived)
+            means = stat_all[n, :, 0, :]
+            mean = jnp.sum(means, axis=0, keepdims=True) / num_rows
+            spread = means - mean
+            square = jnp.sum(stat_all[n, :, 1, :], axis=0, keepdims=True)
+            square = square + count * jnp.sum(spread * spread, axis=0, keepdims=True)
+            variance = square / (count * num_rows)
+            scale = self.gain[...] / jnp.sqrt(variance + 1e-5)
+            centres = [stat_all[n, d, 2:3, :] for d in (1, 0, num_rows - 1)]
+            shifts = [(c - mean) * scale + self.bias[...] for c in centres]
+            rows = jnp.concatenate([scale] + shifts, axis=0)
+            coef_send[n] = rows
+            coef_all[n, 0] = rows
+            for d in range(1, num_cols):
+                self.coef(d).start()
+
+        def ready(self):
+            for d in range(1, num_cols):
+                self.coef(d).wait_recv()
+                pending.append(self.coef(d))
 
     first = Gather(0, field_one, True)
 
@@ -342,82 +412,115 @@
         lax.fori_loop(0, width // unroll, some, 0)
         first.field[k, i + 1] = looked_ref[...].astype(BF16)
 
-    def run_gather(gather, make, early):
-        make(0)
-        gather.own(0)
-        make(3)
-        gather.own(3)
-        make(1)
-        gather.own(1)
+    for i in range(height):
+        look_up(i)
+    pl.semaphore_wait(barrier, num_rows - 1 + num_cols - 1)
+
+    def open_gather(gather, make):
+        for i in (0, 3, 1, 2):
+            make(i)
+            if i != 2:
+                gather.own_right(i)
+            if i != 1:
+                gather.own_left(i)
+            gather.own(i)
+
+    def pass_on(gather):
         gather.from_left(0)
         gather.from_right(3)
-        make(2)
-        gather.own(2)
-        gather.from_right(0)
-        gather.from_left(3)
+        gather.own_right(2)
+        gather.own_left(1)
         if gather.halo:
             gather.halo_in(0)
-        gather.rest(0)
-        early()
         gather.from_left(1)
         gather.from_right(2)
+
+    def pass_more(gather):
+        gather.from_left(3)
+        gather.from_right(0)
+        gather.from_far(0)
+        gather.from_far(3)
+        gather.from_left(2)
+        gather.from_right(1)
         if gather.halo:
             gather.halo_in(1)
             gather.halo_in(2)
-        gather.from_right(1)
-        gather.from_left(2)
-        gather.from_far(0)
-        gather.from_far(3)
-
-    def conv_layer(gather, make, load, weight_ref, n):
-        def early():
-            load.wait()
-            convolve(gather, weight_ref, 0)
-
-        run_gather(gather, make, early)
-        gather.rest(1)
-        convolve(gather, weight_ref, 1)
+
+    def pass_last(gather):
         gather.from_far(1)
         gather.from_far(2)
-        gather.halo_in(3)
-        gather.rest(2)
-        convolve(gather, weight_ref, 2)
-        gather.rest(3)
-        convolve(gather, weight_ref, 3)
-        shifted_sum()
-        return statistics(n)
-
-    mean, variance = conv_layer(first, look_up, loads[1], conv_one_ref, 0)
+        if gather.halo:
+            gather.halo_in(3)
+
+    open_gather(first, lambda i: None)
+    pass_on(first)
+    first.rest(0)
+    loads[1].wait()
+    convolve(field_one, True, conv_one_ref, 0)
+    pass_more(first)
+    first.rest(1)
+    convolve(field_one, True, conv_one_ref, 1)
+    pass_last(first)
+    first.rest(2)
+    convolve(field_one, True, conv_one_ref, 2)
+    first.rest(3)
+    convolve(field_one, True, conv_one_ref, 3)
 
     second = Gather(1, field_two, True)
-    root_one = jnp.sqrt(variance + 1e-5)
-    gain_one = gain_one_ref[...]
-    bias_one = bias_one_ref[...]
-
-    def make_hidden(i):
-        at = slice(i * width, (i + 1) * width)
-        v = (conv_ref[at, :] - mean) / root_one * gain_one + bias_one
-        second.field[k, i + 1] = (v / (1.0 + jnp.exp(-v))).astype(BF16)
-
-    mean_two, variance_two = conv_layer(second, make_hidden, loads[2], conv_two_ref, 1)
+    norm_one = Norm(0, gain_one_ref, bias_one_ref)
+    open_gather(second, lambda i: norm_one.row(i, second))
+    norm_one.tell()
+    pass_on(second)
+    norm_one.settle()
+    pass_more(second)
+    second.rest(0)
+    loads[2].wait()
+    norm_one.ready()
+
+    def part(q):
+        deep = (height + 2) // 2
+        return lambda n: normalise(second, q, [n * deep + j for j in range(deep)])
+
+    def normalise_all(q):
+        def some(n, _):
+            part(q)(n)
+            return 0
+
+        lax.fori_loop(0, 2, some, 0)
+
+    normalise_all(0)
+    convolve(hidden_ref, False, conv_two_ref, 0)
+    pass_last(second)
+    second.rest(1)
+    normalise_all(1)
+    second.rest(2)
+    convolve(hidden_ref, False, conv_two_ref, 1, part(2))
+    second.rest(3)
+    convolve(hidden_ref, False, conv_two_ref, 2, part(3))
+    convolve(hidden_ref, False, conv_two_ref, 3)
 
     third = Gather(2, field_three, False)
-    root_two = jnp.sqrt(variance_two + 1e-5)
-    gain_two = gain_two_ref[...]
-    bias_two = bias_two_ref[...]
-
-    def make_features(i):
-        at = slice(i * width, (i + 1) * width)
-        v = (conv_ref[at, :] - mean_two) / root_two * gain_two + bias_two
-        out = (first.field[k, i + 1].astype(F32) + v).astype(BF16)
-        third.field[k, i] = out
-        features_ref[i] = out
+    norm_two = Norm(1, gain_two_ref, bias_two_ref)
+    open_gather(third, lambda i: norm_two.row(i, third))
+    norm_two.tell()
+    pass_on(third)
+    norm_two.settle()
+    scale_two = coef_all[1, 0, 0:1, :]
+    shift_two = coef_all[1, 0, 2:3, :]
+    for i in range(height):
+        v = conv_ref[i * width : (i + 1) * width, :] * scale_two + shift_two
+        features_ref[i] = (first.field[k, i + 1].astype(F32) + v).astype(BF16)
 
     vocab_here = head_hbm.shape[1]
     tiles = vocab_here // 128
 
     def head_row(i):
-        left_side = jnp.concatenate([third.field[p, i] for p in range(num_cols)], axis=1)
+        columns = []
+        for p in range(num_cols):
+            d = lax.rem(k - p + num_cols, num_cols)
+            v = third.field[p, i].astype(F32) * coef_all[1, d, 0:1, :] + coef_all[1, d, 2:3, :]
+            columns.append((first.field[p, i + 1].astype(F32) + v).astype(BF16))
+        left_side = jnp.concatenate(columns, axis=1)
         logits_ref[...] = jnp.dot(left_side, head_ref[...], preferred_element_type=F32)
         most = logits_ref[:, 0:128]
         for t in range(1, tiles):
@@ -446,17 +549,18 @@
 
         lax.fori_loop(0, 2, one, 0)
 
-    run_gather(third, make_features, lambda: None)
-    for q in range(1, 4):
-        for i in (0, 3):
-            third.wait((OWN, FROM_P, FROM_M, FAR)[q], i, third.owner_of(q, 1 - core), i)
+    def partner_rows(rows):
+        for q in range(4):
+            for i in rows:
+                third.wait((OWN, FROM_P, FROM_M, FAR)[q], i, third.owner_of(q, 1 - core), i)
+
+    pass_more(third)
+    partner_rows((0, 3))
     loads[3].wait()
+    norm_two.ready()
     head_rows(0, 3)
-    third.from_far(1)
-    third.from_far(2)
-    for q in range(1, 4):
-        for i in (1, 2):
-            third.wait((OWN, FROM_P, FROM_M, FAR)[q], i, third.owner_of(q, 1 - core), i)
+    pass_last(third)
+    partner_rows((1, 2))
     head_rows(1, 1)
 
     per_block = num_cols // parts
@@ -556,8 +660,11 @@
             pltpu.VMEM((num_cols, height, width, lanes), BF16),
             pltpu.VMEM((height * width, 3 * lanes), F32),
             pltpu.VMEM((height * width, lanes), F32),
-            pltpu.VMEM((2, 2, lanes), F32),
-            pltpu.VMEM((2, num_rows, 2, lanes), F32),
+            pltpu.VMEM((2, 4, lanes), F32),
+            pltpu.VMEM((2, num_rows, 4, lanes), F32),
+            pltpu.VMEM((2, 4, lanes), F32),
+            pltpu.VMEM((2, num_cols, 4, lanes), F32),
+            pltpu.VMEM((num_cols, height + 2, width, lanes), BF16),
             pltpu.VMEM((width, head_weight.shape[1]), F32),
             pltpu.VMEM((width // 128, 3, height, 128), F32),
             pltpu.VMEM((num_cols, 3, height, 128), F32),
@@ -566,6 +673,8 @@
             pltpu.SemaphoreType.DMA((3, 11, 4)),
             pltpu.SemaphoreType.DMA((2,)),
             pltpu.SemaphoreType.DMA((2,)),
+            pltpu.SemaphoreType.DMA((2, num_cols)),
+            pltpu.SemaphoreType.DMA((2, num_cols)),
             pltpu.SemaphoreType.DMA((num_cols,)),
             pltpu.SemaphoreType.DMA((num_cols,)),
         ],

time: 88.8 us -> 77.5 us (0.87)
  Pallas kernels: 85 us -> 73.8 us
    pallas_call x1, Pallas kernels: 85 us -> 73.8 us  [local(): pl.pallas_call(functools.partial(kernel, num_rows, num_cols), name='denoi...]
where the time goes in v2:
time: 77.5 us; the launch traced here: 77.4 us
  Pallas kernels  73.8 us (95%)
  local copies, waits for them, and re-layouts  2.92 us (4%)
    pallas_call x1, Pallas kernels, local(): pl.pallas_call(functools.partial(kernel, num_rows, num_cols), name='denoi...  73.8 us
    unnamed x2, local copies, waits for them, and re-layouts  2.92 us

profile of v2, /device:TPU:1, one launch (start us, length us, event | category | flops | bytes accessed | tf_op | source)
XLA Modules:
  0.0 77.4 jit_solution(9260704760298123701)
XLA Ops:
  0.6 73.8 %denoise.1 = (bf16[4,256,128]{2,1,0:T(8,128)(2,1)}, f32[4,32]{1,0:T(4,128)}) custom-call(s32[4,256]{1,0:T(4,128)} %ids_ref.1, s32[4,256]{1,0:T(4,128)} %keep_ref.1, s32[8,128]{1,0:T(8,128)} %bitcast.6, bf16[8192,128]{1,0:T(8,128)(2,1)} %table_hbm.1, bf16[1,128]{1,0:T(2,128)(2,1)} %bitcast.7, bf16[3,3,1024,128]{3,2,1,0:T(8,128)(2,1)} %conv_one_hbm.1, ...), custom_call_target="tpu_custom_call" | custom-call | tf_op jit(solution)/shard_map/denoise/pallas_call | solution.py:626
  74.4 1.7 %copy.16 = bf16[4,256,128]{2,1,0:T(8,128)(2,1)} copy(bf16[4,256,128]{2,1,0:T(8,128)(2,1)} %get-tuple-element.4) | data formatting | bytes 524288
  76.1 1.2 %copy.17 = f32[4,32]{1,0:T(4,128)} copy(f32[4,32]{1,0:T(4,128)} %get-tuple-element.5) | data formatting | bytes 1024

commit v3 on v2

--- a/solution.py
+++ b/solution.py
@@ -61,6 +61,7 @@
     coef_send,
     coef_all,
     hidden_ref,
+    rows_ref,
     logits_ref,
     last_send,
     last_all,
@@ -73,6 +74,7 @@
     coef_recv_sems,
     last_send_sems,
     last_recv_sems,
+    known_sems,
 ):
     height, width = ids_ref.shape
     vocab = table_hbm.shape[0]
@@ -103,31 +105,32 @@
             )
         )
     ]
-    for load in loads:
-        load.start()
+    loads[0].start()
 
     barrier = pltpu.get_barrier_semaphore()
 
-    def greet_row(d, _):
-        pl.semaphore_signal(
-            barrier,
-            inc=1,
-            device_id={"rows": lax.rem(r + d, num_rows)},
-            device_id_type=MESH,
-        )
-        return 0
-
-    def greet_col(d, _):
-        pl.semaphore_signal(
-            barrier,
-            inc=1,
-            device_id={"cols": lax.rem(k + d, num_cols)},
-            device_id_type=MESH,
-        )
-        return 0
-
-    lax.fori_loop(1, num_rows, greet_row, 0)
-    lax.fori_loop(1, num_cols, greet_col, 0)
+    def greet(device):
+        pl.semaphore_signal(barrier, inc=1, device_id=device, device_id_type=MESH)
+
+    for d in range(1, num_cols):
+        greet({"cols": lax.rem(k + d, num_cols)})
+    greet({"rows": above})
+    greet({"rows": below})
+
+    def tell_known(m):
+        far = 2**m
+        for to in (lax.rem(r + far, num_rows), lax.rem(r + num_rows - far, num_rows)):
+            pl.semaphore_signal(
+                known_sems.at[m], inc=1, device_id={"rows": to}, device_id_type=MESH
+            )
+
+    rounds = max(num_rows.bit_length() - 2, 0)
+
+    def meet(m):
+        if m < rounds:
+            pl.semaphore_wait(known_sems.at[m], 2)
+            if m + 1 < rounds:
+                tell_known(m + 1)
 
     half = height * width * num_rows // 2
     parts = width // 128
@@ -139,10 +142,15 @@
             ids_vmem[n : n + 1, :] = jnp.where(visible, ids_ref[at], vocab)
     to_smem = pltpu.make_async_copy(ids_vmem, ids_smem, load_sems.at[4])
     to_smem.start()
-    for i in range(height):
-        row = ids_ref[i : i + 1, :].astype(F32)
-        tokens_ref[i] = jnp.broadcast_to(row, (128, width)).T
+
+    def lay_tokens():
+        for i in range(height):
+            row = ids_ref[i : i + 1, :].astype(F32)
+            tokens_ref[i] = jnp.broadcast_to(row, (128, width)).T
+
     loads[0].wait()
+    for load in loads[1:]:
+        load.start()
     step_rows = 512
 
     def widen(n, _):
@@ -231,13 +239,19 @@
             self.wait(DOWN, q, owner, 0)
             self.send(DOWNF, q, owner, 0, {"cols": partner})
 
+        def rest_rows(self, q, rows):
+            owner = self.owner_of(q, 1 - core)
+            for i in rows:
+                self.wait((OWN, FROM_P, FROM_M, FAR)[q], i, owner, i + self.off)
+
+        def rest_halo(self, q):
+            owner = self.owner_of(q, 1 - core)
+            self.wait(UPF, q, owner, height + 1)
+            self.wait(DOWNF, q, owner, 0)
+
         def rest(self, q):
-            owner = self.owner_of(q, 1 - core)
-            for i in range(height):
-                self.wait((OWN, FROM_P, FROM_M, FAR)[q], i, owner, i + self.off)
-            if self.halo:
-                self.wait(UPF, q, owner, height + 1)
-                self.wait(DOWNF, q, owner, 0)
+            self.rest_rows(q, range(height))
+            self.rest_halo(q)
 
     def at_chip(q):
         return lax.rem(chip + (0, chips - 1, 1, 2)[q], chips)
@@ -258,9 +272,8 @@
                 v = v + v * jnp.tanh(v)
                 hidden_ref[owner, slot] = jnp.where(inside, v, 0.0).astype(BF16)
 
-    def convolve(field, masked, weight_ref, q, beside=None):
+    def convolve(field, masked, weight_ref, q, outs, started=True):
         at = at_chip(q)
-        one, two = at * 2, at * 2 + 1
         rows = pl.ds(pl.multiple_of(at * 2 * lanes, 2 * lanes), 2 * lanes)
         weights = jnp.concatenate(
             [
@@ -269,34 +282,28 @@
             ],
             axis=0,
         )
-        tall = 2
-
-        def block(n, _):
-            first = n * tall
-            keep_up = jnp.logical_or(r > 0, n > 0)
-            keep_down = jnp.logical_or(r < num_rows - 1, n < height // tall - 1)
-            columns = []
-            for a in range(3):
-                for p in (one, two):
-                    tiles = [field[p, first + a + t] for t in range(tall)]
-                    if masked and a == 0:
-                        tiles[0] = jnp.where(keep_up, tiles[0], jnp.zeros_like(tiles[0]))
-                    if masked and a == 2:
-                        tiles[-1] = jnp.where(keep_down, tiles[-1], jnp.zeros_like(tiles[-1]))
-                    columns.append(jnp.concatenate(tiles, axis=0))
-            product = jnp.dot(
-                jnp.concatenate(columns, axis=1), weights, preferred_element_type=F32
-            )
-            at_rows = pl.ds(pl.multiple_of(first * width, tall * width), tall * width)
-            if q == 0:
-                total_ref[at_rows, :] = product
+        columns = []
+        for a in range(3):
+            for p in (at * 2, at * 2 + 1):
+                tiles = []
+                for i in outs:
+                    tile = field[p, i + a]
+                    if masked and i + a == 0:
+                        tile = jnp.where(r > 0, tile, jnp.zeros_like(tile))
+                    if masked and i + a == height + 1:
+                        tile = jnp.where(r < num_rows - 1, tile, jnp.zeros_like(tile))
+                    tiles.append(tile)
+                columns.append(jnp.concatenate(tiles, axis=0))
+        product = jnp.dot(
+            jnp.concatenate(columns, axis=1), weights, preferred_element_type=F32
+        )
+        for n, i in enumerate(outs):
+            here = slice(i * width, (i + 1) * width)
+            part = product[n * width : (n + 1) * width]
+            if started:
+                total_ref[here, :] += part
             else:
-                total_ref[at_rows, :] += product
-            if beside is not None:
-                beside(n)
-            return 0
-
-        lax.fori_loop(0, height // tall, block, 0)
+                total_ref[here, :] = part
 
     def shifted_row(i):
         index = lax.broadcasted_iota(jnp.int32, (width, lanes), 0)
@@ -412,9 +419,10 @@
         lax.fori_loop(0, width // unroll, some, 0)
         first.field[k, i + 1] = looked_ref[...].astype(BF16)
 
-    for i in range(height):
-        look_up(i)
-    pl.semaphore_wait(barrier, num_rows - 1 + num_cols - 1)
+    look_up(0)
+    pl.semaphore_wait(barrier, num_cols - 1 + 2)
+    if rounds > 0:
+        tell_known(0)
 
     def open_gather(gather, make):
         for i in (0, 3, 1, 2):
@@ -435,36 +443,39 @@
         gather.from_left(1)
         gather.from_right(2)
 
-    def pass_more(gather):
-        gather.from_left(3)
-        gather.from_right(0)
-        gather.from_far(0)
-        gather.from_far(3)
-        gather.from_left(2)
-        gather.from_right(1)
-        if gather.halo:
-            gather.halo_in(1)
-            gather.halo_in(2)
-
-    def pass_last(gather):
-        gather.from_far(1)
-        gather.from_far(2)
-        if gather.halo:
-            gather.halo_in(3)
-
-    open_gather(first, lambda i: None)
+    inner, outer, every = (1, 2), (0, 3), (0, 1, 2, 3)
+
+    open_gather(first, lambda i: look_up(i) if i > 0 else None)
     pass_on(first)
+    meet(0)
+    lay_tokens()
     first.rest(0)
     loads[1].wait()
-    convolve(field_one, True, conv_one_ref, 0)
-    pass_more(first)
-    first.rest(1)
-    convolve(field_one, True, conv_one_ref, 1)
-    pass_last(first)
-    first.rest(2)
-    convolve(field_one, True, conv_one_ref, 2)
+    convolve(field_one, True, conv_one_ref, 0, every, False)
+    meet(1)
+    first.from_left(3)
+    first.from_right(0)
+    first.from_far(0)
+    first.from_far(3)
+    meet(2)
+    first.from_left(2)
+    first.from_right(1)
+    first.halo_in(1)
+    first.halo_in(2)
+    meet(3)
+    first.rest_rows(1, every)
+    convolve(field_one, True, conv_one_ref, 1, inner)
+    first.from_far(1)
+    first.from_far(2)
+    first.rest_rows(2, every)
+    convolve(field_one, True, conv_one_ref, 2, inner)
+    first.halo_in(3)
+    first.rest_halo(1)
+    convolve(field_one, True, conv_one_ref, 1, outer)
+    first.rest_halo(2)
+    convolve(field_one, True, conv_one_ref, 2, outer)
     first.rest(3)
-    convolve(field_one, True, conv_one_ref, 3)
+    convolve(field_one, True, conv_one_ref, 3, every)
 
     second = Gather(1, field_two, True)
     norm_one = Norm(0, gain_one_ref, bias_one_ref)
@@ -472,32 +483,32 @@
     norm_one.tell()
     pass_on(second)
     norm_one.settle()
-    pass_more(second)
+    second.from_left(3)
+    second.from_right(0)
+    second.from_far(0)
+    second.from_far(3)
+    second.from_left(2)
+    second.from_right(1)
+    second.halo_in(1)
+    second.halo_in(2)
     second.rest(0)
     loads[2].wait()
     norm_one.ready()
-
-    def part(q):
-        deep = (height + 2) // 2
-        return lambda n: normalise(second, q, [n * deep + j for j in range(deep)])
-
-    def normalise_all(q):
-        def some(n, _):
-            part(q)(n)
-            return 0
-
-        lax.fori_loop(0, 2, some, 0)
-
-    normalise_all(0)
-    convolve(hidden_ref, False, conv_two_ref, 0)
-    pass_last(second)
+    slots = range(height + 2)
+    normalise(second, 0, slots)
+    second.from_far(1)
+    second.from_far(2)
     second.rest(1)
-    normalise_all(1)
+    normalise(second, 1, slots)
+    convolve(hidden_ref, False, conv_two_ref, 0, every, False)
+    second.halo_in(3)
     second.rest(2)
-    convolve(hidden_ref, False, conv_two_ref, 1, part(2))
+    normalise(second, 2, slots)
+    convolve(hidden_ref, False, conv_two_ref, 1, every)
     second.rest(3)
-    convolve(hidden_ref, False, conv_two_ref, 2, part(3))
-    convolve(hidden_ref, False, conv_two_ref, 3)
+    normalise(second, 3, slots)
+    convolve(hidden_ref, False, conv_two_ref, 2, every)
+    convolve(hidden_ref, False, conv_two_ref, 3, every)
 
     third = Gather(2, field_three, False)
     norm_two = Norm(1, gain_two_ref, bias_two_ref)
@@ -514,54 +525,63 @@
     vocab_here = head_hbm.shape[1]
     tiles = vocab_here // 128
 
-    def head_row(i):
-        columns = []
+    def all_features(i, to):
         for p in range(num_cols):
             d = lax.rem(k - p + num_cols, num_cols)
             v = third.field[p, i].astype(F32) * coef_all[1, d, 0:1, :] + coef_all[1, d, 2:3, :]
-            columns.append((first.field[p, i + 1].astype(F32) + v).astype(BF16))
-        left_side = jnp.concatenate(columns, axis=1)
-        logits_ref[...] = jnp.dot(left_side, head_ref[...], preferred_element_type=F32)
-        most = logits_ref[:, 0:128]
+            v = first.field[p, i + 1].astype(F32) + v
+            rows_ref[to, :, p * lanes : (p + 1) * lanes] = v.astype(BF16)
+
+    def row_logits(to):
+        logits_ref[to] = jnp.dot(rows_ref[to], head_ref[...], preferred_element_type=F32)
+
+    def row_totals(i, to):
+        most = logits_ref[to, :, 0:128]
         for t in range(1, tiles):
-            most = jnp.maximum(most, logits_ref[:, 128 * t : 128 * t + 128])
+            most = jnp.maximum(most, logits_ref[to, :, 128 * t : 128 * t + 128])
         top = jnp.max(most, axis=1, keepdims=True)
         token = tokens_ref[i]
         lane = lax.broadcasted_iota(jnp.int32, (width, 128), 1)
         summed = jnp.zeros((width, 128), F32)
         picked = jnp.zeros((width, 128), F32)
         for t in range(tiles):
-            part = logits_ref[:, 128 * t : 128 * t + 128]
+            part = logits_ref[to, :, 128 * t : 128 * t + 128]
             summed = summed + jnp.exp(part - top)
             ids = (lane + (k * vocab_here + 128 * t)).astype(F32)
             picked = picked + jnp.where(ids == token, part, 0.0)
         top_row = jnp.max(most.T, axis=0, keepdims=True)
         sum_row = jnp.sum(summed.T, axis=0, keepdims=True)
         pick_row = jnp.sum(picked.T, axis=0, keepdims=True)
-        for s, row in enumerate((top_row, sum_row, pick_row)):
+        for n, row in enumerate((top_row, sum_row, pick_row)):
             for b in range(parts):
-                last_send[b, s, pl.ds(i, 1), :] = row[:, 128 * b : 128 * b + 128]
-
-    def head_rows(start, step):
-        def one(n, _):
-            head_row(start + step * n)
-            return 0
-
-        lax.fori_loop(0, 2, one, 0)
-
-    def partner_rows(rows):
-        for q in range(4):
-            for i in rows:
-                third.wait((OWN, FROM_P, FROM_M, FAR)[q], i, third.owner_of(q, 1 - core), i)
-
-    pass_more(third)
-    partner_rows((0, 3))
+                last_send[b, n, i : i + 1, :] = row[:, 128 * b : 128 * b + 128]
+
+    third.from_left(3)
+    third.from_right(0)
+    third.from_far(0)
+    third.from_far(3)
+    third.from_left(2)
+    third.from_right(1)
+    for q in range(4):
+        third.rest_rows(q, (0, 3))
     loads[3].wait()
     norm_two.ready()
-    head_rows(0, 3)
-    pass_last(third)
-    partner_rows((1, 2))
-    head_rows(1, 1)
+    all_features(0, 0)
+    row_logits(0)
+    all_features(3, 1)
+    third.from_far(1)
+    third.from_far(2)
+    row_logits(1)
+    row_totals(0, 0)
+    for q in range(4):
+        third.rest_rows(q, (1, 2))
+    all_features(1, 0)
+    row_logits(0)
+    row_totals(3, 1)
+    all_features(2, 1)
+    row_logits(1)
+    row_totals(1, 0)
+    row_totals(2, 1)
 
     per_block = num_cols // parts
 
@@ -665,7 +685,8 @@
             pltpu.VMEM((2, 4, lanes), F32),
             pltpu.VMEM((2, num_cols, 4, lanes), F32),
             pltpu.VMEM((num_cols, height + 2, width, lanes), BF16),
-            pltpu.VMEM((width, head_weight.shape[1]), F32),
+            pltpu.VMEM((2, width, num_cols * lanes), BF16),
+            pltpu.VMEM((2, width, head_weight.shape[1]), F32),
             pltpu.VMEM((width // 128, 3, height, 128), F32),
             pltpu.VMEM((num_cols, 3, height, 128), F32),
             pltpu.SemaphoreType.DMA((5,)),
@@ -677,6 +698,7 @@
             pltpu.SemaphoreType.DMA((2, num_cols)),
             pltpu.SemaphoreType.DMA((num_cols,)),
             pltpu.SemaphoreType.DMA((num_cols,)),
+            pltpu.SemaphoreType.REGULAR((8,)),
         ],
         compiler_params=pltpu.CompilerParams(
             collective_id=0, has_side_effects=True, vmem_limit_bytes=60 * 1024 * 1024

time: 77.5 us -> 75.2 us (0.970)
  Pallas kernels: 73.8 us -> 71.4 us
    pallas_call x1, Pallas kernels: 73.8 us -> 71.4 us  [local(): pl.pallas_call(functools.partial(kernel, num_rows, num_cols), name='denoi...]
where the time goes in v3:
time: 75.2 us; the launch traced here: 75 us
  Pallas kernels  71.4 us (95%)
  local copies, waits for them, and re-layouts  2.92 us (4%)
    pallas_call x1, Pallas kernels, local(): pl.pallas_call(functools.partial(kernel, num_rows, num_cols), name='denoi...  71.4 us
    unnamed x2, local copies, waits for them, and re-layouts  2.92 us

profile of v3, /device:TPU:1, one launch (start us, length us, event | category | flops | bytes accessed | tf_op | source)
XLA Modules:
  0.0 75.0 jit_solution(12238496062871932023)
XLA Ops:
  0.6 71.4 %denoise.1 = (bf16[4,256,128]{2,1,0:T(8,128)(2,1)}, f32[4,32]{1,0:T(4,128)}) custom-call(s32[4,256]{1,0:T(4,128)} %ids_ref.1, s32[4,256]{1,0:T(4,128)} %keep_ref.1, s32[8,128]{1,0:T(8,128)} %bitcast.6, bf16[8192,128]{1,0:T(8,128)(2,1)} %table_hbm.1, bf16[1,128]{1,0:T(2,128)(2,1)} %bitcast.7, bf16[3,3,1024,128]{3,2,1,0:T(8,128)(2,1)} %conv_one_hbm.1, ...), custom_call_target="tpu_custom_call" | custom-call | tf_op jit(solution)/shard_map/denoise/pallas_call | solution.py:646
  72.1 1.7 %copy.16 = bf16[4,256,128]{2,1,0:T(8,128)(2,1)} copy(bf16[4,256,128]{2,1,0:T(8,128)(2,1)} %get-tuple-element.4) | data formatting | bytes 524288
  73.7 1.2 %copy.17 = f32[4,32]{1,0:T(4,128)} copy(f32[4,32]{1,0:T(4,128)} %get-tuple-element.5) | data formatting | bytes 1024

commit v4 on v3

--- a/solution.py
+++ b/solution.py
@@ -41,7 +41,7 @@
     bias_two_ref,
     head_hbm,
     features_ref,
-    logp_ref,
+    totals_ref,
     table_ref,
     wide_ref,
     conv_one_ref,
@@ -197,9 +197,7 @@
                 self.send(DOWN, q, owner, height, {"rows": below}, to_row=0)
 
         def own(self, i):
-            row = i + self.off
-            self.halo_out(0, k, i)
-            self.send(OWN, i, k, row, {"cols": partner})
+            self.send(OWN, i, k, i + self.off, {"cols": partner})
 
         def own_right(self, i):
             self.send(XP, i, k, i + self.off, {"cols": right})
@@ -397,9 +395,16 @@
             for d in range(1, num_cols):
                 self.coef(d).start()
 
-        def ready(self):
+        def ready(self, q):
+            for c in range(2):
+                if q == 0 and c == 1:
+                    continue
+                owner = partner if q == 0 else at_chip(q) * 2 + c
+                arrived = self.coef(lax.rem(k - owner + num_cols, num_cols))
+                arrived.wait_recv()
+
+        def sent(self):
             for d in range(1, num_cols):
-                self.coef(d).wait_recv()
                 pending.append(self.coef(d))
 
     first = Gather(0, field_one, True)
@@ -424,45 +429,54 @@
     if rounds > 0:
         tell_known(0)
 
-    def open_gather(gather, make):
+    def open_gather(gather):
+        for i, j in ((0, 3), (1, 2), (3, 0)):
+            gather.own_right(i)
+            gather.own_left(j)
         for i in (0, 3, 1, 2):
-            make(i)
-            if i != 2:
-                gather.own_right(i)
-            if i != 1:
-                gather.own_left(i)
             gather.own(i)
 
-    def pass_on(gather):
+    def pass_first(gather):
         gather.from_left(0)
         gather.from_right(3)
         gather.own_right(2)
         gather.own_left(1)
-        if gather.halo:
-            gather.halo_in(0)
-        gather.from_left(1)
-        gather.from_right(2)
 
     inner, outer, every = (1, 2), (0, 3), (0, 1, 2, 3)
 
-    open_gather(first, lambda i: look_up(i) if i > 0 else None)
-    pass_on(first)
+    first.own_right(0)
+    first.halo_out(0, k, 0)
+    first.own(0)
+    look_up(3)
+    first.own_left(3)
+    first.halo_out(0, k, 3)
+    first.own(3)
+    look_up(1)
+    first.own_right(1)
+    first.own(1)
+    look_up(2)
+    first.own_left(2)
+    first.own(2)
+    first.own_right(3)
+    first.own_left(0)
+    pass_first(first)
+    first.halo_in(0)
     meet(0)
+    first.from_left(1)
+    first.from_right(2)
     lay_tokens()
     first.rest(0)
     loads[1].wait()
     convolve(field_one, True, conv_one_ref, 0, every, False)
-    meet(1)
     first.from_left(3)
     first.from_right(0)
     first.from_far(0)
     first.from_far(3)
-    meet(2)
+    meet(1)
     first.from_left(2)
     first.from_right(1)
     first.halo_in(1)
     first.halo_in(2)
-    meet(3)
     first.rest_rows(1, every)
     convolve(field_one, True, conv_one_ref, 1, inner)
     first.from_far(1)
@@ -470,6 +484,7 @@
     first.rest_rows(2, every)
     convolve(field_one, True, conv_one_ref, 2, inner)
     first.halo_in(3)
+    meet(2)
     first.rest_halo(1)
     convolve(field_one, True, conv_one_ref, 1, outer)
     first.rest_halo(2)
@@ -479,43 +494,59 @@
 
     second = Gather(1, field_two, True)
     norm_one = Norm(0, gain_one_ref, bias_one_ref)
-    open_gather(second, lambda i: norm_one.row(i, second))
+    for i in (0, 3, 1, 2):
+        norm_one.row(i, second)
+    open_gather(second)
+    meet(3)
     norm_one.tell()
-    pass_on(second)
+    second.halo_out(0, k, 0)
+    second.halo_out(0, k, 3)
+    pass_first(second)
+    second.halo_in(0)
     norm_one.settle()
+    second.from_left(1)
+    second.from_right(2)
     second.from_left(3)
     second.from_right(0)
     second.from_far(0)
     second.from_far(3)
+    second.rest(0)
+    loads[2].wait()
+    norm_one.ready(0)
+    slots = range(height + 2)
+    normalise(second, 0, slots)
+    convolve(hidden_ref, False, conv_two_ref, 0, every, False)
     second.from_left(2)
     second.from_right(1)
     second.halo_in(1)
     second.halo_in(2)
-    second.rest(0)
-    loads[2].wait()
-    norm_one.ready()
-    slots = range(height + 2)
-    normalise(second, 0, slots)
     second.from_far(1)
     second.from_far(2)
+    norm_one.ready(1)
     second.rest(1)
     normalise(second, 1, slots)
-    convolve(hidden_ref, False, conv_two_ref, 0, every, False)
     second.halo_in(3)
+    norm_one.ready(2)
     second.rest(2)
     normalise(second, 2, slots)
     convolve(hidden_ref, False, conv_two_ref, 1, every)
+    norm_one.ready(3)
     second.rest(3)
     normalise(second, 3, slots)
     convolve(hidden_ref, False, conv_two_ref, 2, every)
     convolve(hidden_ref, False, conv_two_ref, 3, every)
+    norm_one.sent()
 
     third = Gather(2, field_three, False)
     norm_two = Norm(1, gain_two_ref, bias_two_ref)
-    open_gather(third, lambda i: norm_two.row(i, third))
+    for i in (0, 3, 1, 2):
+        norm_two.row(i, third)
+    open_gather(third)
     norm_two.tell()
-    pass_on(third)
+    pass_first(third)
     norm_two.settle()
+    third.from_left(1)
+    third.from_right(2)
     scale_two = coef_all[1, 0, 0:1, :]
     shift_two = coef_all[1, 0, 2:3, :]
     for i in range(height):
@@ -565,7 +596,9 @@
     for q in range(4):
         third.rest_rows(q, (0, 3))
     loads[3].wait()
-    norm_two.ready()
+    for q in range(4):
+        norm_two.ready(q)
+    norm_two.sent()
     all_features(0, 0)
     row_logits(0)
     all_features(3, 1)
@@ -601,6 +634,18 @@
     last_all[0] = last_send[k // per_block]
     for d in range(1, num_cols):
         exchange(d).wait_recv()
+    totals_ref[...] = last_all[...]
+
+    for copy in pending:
+        copy.wait_send()
+    for d in range(1, num_cols):
+        exchange(d).wait_send()
+
+
+def finish(num_cols, made_ref, last_all, features_ref, logp_ref):
+    features_ref[...] = made_ref[...]
+    per_block = num_cols // (made_ref.shape[1] // 128)
+    mine = made_ref.shape[1] // num_cols
     top = last_all[0, 0]
     for d in range(1, num_cols):
         top = jnp.maximum(top, last_all[d, 0])
@@ -610,17 +655,11 @@
         summed = summed + last_all[d, 1] * jnp.exp(last_all[d, 0] - top)
         picked = picked + last_all[d, 2]
     logp = picked - top - jnp.log(summed)
-    mine = width // num_cols
-    place = lax.rem(k, per_block)
+    place = lax.rem(lax.axis_index("cols"), per_block)
     out = logp[:, 0:mine]
     for b in range(1, per_block):
         out = jnp.where(place == b, logp[:, mine * b : mine * b + mine], out)
     logp_ref[...] = out
-
-    for copy in pending:
-        copy.wait_send()
-    for d in range(1, num_cols):
-        exchange(d).wait_send()
 
 
 def local(
@@ -643,12 +682,12 @@
     lines = height * width // 128
     in_vmem = pl.BlockSpec(memory_space=pltpu.VMEM)
     anywhere = pl.BlockSpec(memory_space=pl.ANY)
-    return pl.pallas_call(
+    made, totals = pl.pallas_call(
         functools.partial(kernel, num_rows, num_cols),
         name="denoise",
         out_shape=(
             jax.ShapeDtypeStruct((height, width, lanes), BF16),
-            jax.ShapeDtypeStruct((height, width // num_cols), F32),
+            jax.ShapeDtypeStruct((num_cols, 3, height, 128), F32),
         ),
         in_specs=[
             in_vmem,
@@ -717,6 +756,16 @@
         bias_two.reshape(1, lanes),
         head_weight,
     )
+    return pl.pallas_call(
+        functools.partial(finish, num_cols),
+        name="finish",
+        out_shape=(
+            jax.ShapeDtypeStruct((height, width, lanes), BF16),
+            jax.ShapeDtypeStruct((height, width // num_cols), F32),
+        ),
+        in_specs=[in_vmem, in_vmem],
+        out_specs=(in_vmem, in_vmem),
+    )(made, totals)
 
 
 def solution(mesh):

time: 75.2 us -> 69.5 us (0.924)
  local copies, waits for them, and re-layouts: 2.92 us -> 0 us
  Pallas kernels: 71.4 us -> 68.7 us
    pallas_call x1, Pallas kernels: 71.4 us -> 66.8 us  [local(): pl.pallas_call(functools.partial(kernel, num_rows, num_cols), name='denoi...]
    unnamed x2 -> x0, local copies, waits for them, and re-layouts: 2.92 us -> none
    pallas_call x0 -> x1, Pallas kernels: none -> 1.9 us  [local(): pl.pallas_call(functools.partial(finish, num_cols), name='finish', out_sh...]
where the time goes in v4:
time: 69.5 us; the launch traced here: 69.3 us
  Pallas kernels  68.7 us (99%)
    pallas_call x1, Pallas kernels, local(): pl.pallas_call(functools.partial(kernel, num_rows, num_cols), name='denoi...  66.8 us
    pallas_call x1, Pallas kernels, local(): pl.pallas_call(functools.partial(finish, num_cols), name='finish', out_sh...  1.9 us

profile of v4, /device:TPU:1, one launch (start us, length us, event | category | flops | bytes accessed | tf_op | source)
XLA Modules:
  0.0 69.3 jit_solution(15033076903460236453)
XLA Ops:
  0.6 66.8 %denoise.1 = (bf16[4,256,128]{2,1,0:T(8,128)(2,1)}, f32[8,3,4,128]{3,2,1,0:T(4,128)}) custom-call(s32[4,256]{1,0:T(4,128)} %ids_ref.1, s32[4,256]{1,0:T(4,128)} %keep_ref.1, s32[8,128]{1,0:T(8,128)} %bitcast.6, bf16[8192,128]{1,0:T(8,128)(2,1)} %table_hbm.1, bf16[1,128]{1,0:T(2,128)(2,1)} %bitcast.7, bf16[3,3,1024,128]{3,2,1,0:T(8,128)(2,1)} %conv_one_hbm.1, ...), custom_call_target="tpu_custom_call" | custom-call | tf_op jit(solution)/shard_map/denoise/pallas_call | solution.py:685
  67.4 1.9 %finish.1 = (bf16[4,256,128]{2,1,0:T(8,128)(2,1)}, f32[4,32]{1,0:T(4,128)}) custom-call(bf16[4,256,128]{2,1,0:T(8,128)(2,1)} %get-tuple-element.4.made_ref, f32[8,3,4,128]{3,2,1,0:T(4,128)} %get-tuple-element.5.last_all), custom_call_target="tpu_custom_call" | custom-call | tf_op jit(solution)/shard_map/finish/pallas_call | solution.py:759

commit v5 on v4

--- a/solution.py
+++ b/solution.py
@@ -28,20 +28,29 @@
 def kernel(
     num_rows,
     num_cols,
+    ids_hbm,
+    keep_hbm,
+    order_hbm,
+    table_hbm,
+    mask_hbm,
+    conv_one_hbm,
+    gain_one_hbm,
+    bias_one_hbm,
+    conv_two_hbm,
+    gain_two_hbm,
+    bias_two_hbm,
+    head_hbm,
+    features_hbm,
+    totals_ref,
     ids_ref,
     keep_ref,
     order_ref,
-    table_hbm,
     mask_ref,
-    conv_one_hbm,
     gain_one_ref,
     bias_one_ref,
-    conv_two_hbm,
     gain_two_ref,
     bias_two_ref,
-    head_hbm,
     features_ref,
-    totals_ref,
     table_ref,
     wide_ref,
     conv_one_ref,
@@ -62,6 +71,7 @@
     coef_all,
     hidden_ref,
     rows_ref,
+    early_ref,
     logits_ref,
     last_send,
     last_all,
@@ -76,7 +86,7 @@
     last_recv_sems,
     known_sems,
 ):
-    height, width = ids_ref.shape
+    height, width = ids_hbm.shape
     vocab = table_hbm.shape[0]
     lanes = table_hbm.shape[1]
     channels = num_cols * lanes
@@ -94,18 +104,30 @@
     above = lax.rem(r + num_rows - 1, num_rows)
     below = lax.rem(r + 1, num_rows)
 
+    chunks = 4
+    deep = vocab // chunks
+    moves = [
+        (ids_hbm, ids_ref),
+        (keep_hbm, keep_ref),
+        (order_hbm, order_ref),
+        (mask_hbm, mask_ref),
+    ]
+    moves += [(table_hbm.at[pl.ds(n * deep, deep)], table_ref.at[pl.ds(n * deep, deep)]) for n in range(chunks)]
+    moves += [
+        (conv_one_hbm, conv_one_ref),
+        (conv_two_hbm, conv_two_ref),
+        (head_hbm, head_ref),
+        (gain_one_hbm, gain_one_ref),
+        (bias_one_hbm, bias_one_ref),
+        (gain_two_hbm, gain_two_ref),
+        (bias_two_hbm, bias_two_ref),
+    ]
     loads = [
-        pltpu.make_async_copy(src, dst, load_sems.at[n])
-        for n, (src, dst) in enumerate(
-            (
-                (table_hbm, table_ref),
-                (conv_one_hbm, conv_one_ref),
-                (conv_two_hbm, conv_two_ref),
-                (head_hbm, head_ref),
-            )
-        )
+        pltpu.make_async_copy(src, dst, load_sems.at[n]) for n, (src, dst) in enumerate(moves)
     ]
-    loads[0].start()
+    lookup_loads, table_loads, late_loads = loads[:4], loads[4 : 4 + chunks], loads[4 + chunks :]
+    for load in lookup_loads + table_loads:
+        load.start()
 
     barrier = pltpu.get_barrier_semaphore()
 
@@ -132,6 +154,8 @@
             if m + 1 < rounds:
                 tell_known(m + 1)
 
+    for load in lookup_loads:
+        load.wait()
     half = height * width * num_rows // 2
     parts = width // 128
     for i in range(height):
@@ -140,26 +164,27 @@
             n = i * parts + j
             visible = (keep_ref[at] == 1) | (order_ref[n : n + 1, :] >= half)
             ids_vmem[n : n + 1, :] = jnp.where(visible, ids_ref[at], vocab)
-    to_smem = pltpu.make_async_copy(ids_vmem, ids_smem, load_sems.at[4])
+    to_smem = pltpu.make_async_copy(ids_vmem, ids_smem, load_sems.at[len(moves)])
     to_smem.start()
+    wide_ref[vocab : vocab + 8, :] = jnp.broadcast_to(mask_ref[...].astype(F32), (8, lanes))
 
     def lay_tokens():
         for i in range(height):
             row = ids_ref[i : i + 1, :].astype(F32)
             tokens_ref[i] = jnp.broadcast_to(row, (128, width)).T
 
-    loads[0].wait()
-    for load in loads[1:]:
+    step_rows = 512
+    for n in range(chunks):
+        table_loads[n].wait()
+
+        def widen(m, _, n=n):
+            at = pl.ds(pl.multiple_of(n * deep + m * step_rows, step_rows), step_rows)
+            wide_ref[at, :] = table_ref[at, :].astype(F32)
+            return 0
+
+        lax.fori_loop(0, deep // step_rows, widen, 0)
+    for load in late_loads:
         load.start()
-    step_rows = 512
-
-    def widen(n, _):
-        at = pl.ds(pl.multiple_of(n * step_rows, step_rows), step_rows)
-        wide_ref[at, :] = table_ref[at, :].astype(F32)
-        return 0
-
-    lax.fori_loop(0, vocab // step_rows, widen, 0)
-    wide_ref[vocab : vocab + 8, :] = jnp.broadcast_to(mask_ref[...].astype(F32), (8, lanes))
     to_smem.wait()
 
     pending = []
@@ -317,6 +342,23 @@
     positions = height * width
     count = positions * GROUP_WIDTH
 
+    deep_z = min(8, num_rows)
+    deep_y = num_rows // deep_z
+
+    def row_at(d):
+        y = lax.rem(r // deep_z + d // deep_z, deep_y)
+        return y * deep_z + lax.rem(lax.rem(r, deep_z) + d % deep_z, deep_z)
+
+    def hops(d):
+        y, z = d // deep_z, d % deep_z
+        return min(y, deep_y - y) + min(z, deep_z - z)
+
+    far_first = sorted(range(1, num_rows), key=hops, reverse=True)
+    at_start = jnp.where(lax.rem(r, deep_z) == 0, 1, 0)
+    at_end = jnp.where(lax.rem(r, deep_z) == deep_z - 1, 1, 0)
+    slot_above = lax.rem(1 + deep_z * at_start, num_rows)
+    slot_below = deep_z - 1 + deep_z * (deep_y - 1) * at_end
+
     class Norm:
         def __init__(self, n, gain, bias):
             self.n, self.gain, self.bias = n, gain, bias
@@ -343,18 +385,15 @@
             stat_send[n] = both
             stat_all[n, 0] = both
 
-            def one(d, _):
+            for d in far_first:
                 pltpu.make_async_remote_copy(
                     src_ref=stat_send.at[n],
                     dst_ref=stat_all.at[n, d],
                     send_sem=stat_send_sems.at[n],
                     recv_sem=stat_recv_sems.at[n],
-                    device_id={"rows": lax.rem(r + d, num_rows)},
+                    device_id={"rows": row_at(d)},
                     device_id_type=MESH,
                 ).start()
-                return 0
-
-            lax.fori_loop(1, num_rows, one, 0)
 
         def coef(self, d):
             n = self.n
@@ -387,7 +426,7 @@
             square = square + count * jnp.sum(spread * spread, axis=0, keepdims=True)
             variance = square / (count * num_rows)
             scale = self.gain[...] / jnp.sqrt(variance + 1e-5)
-            centres = [stat_all[n, d, 2:3, :] for d in (1, 0, num_rows - 1)]
+            centres = [stat_all[n, d, 2:3, :] for d in (slot_above, 0, slot_below)]
             shifts = [(c - mean) * scale + self.bias[...] for c in centres]
             rows = jnp.concatenate([scale] + shifts, axis=0)
             coef_send[n] = rows
@@ -410,7 +449,7 @@
     first = Gather(0, field_one, True)
 
     def look_up(i):
-        unroll = 16
+        unroll = 64
 
         def some(n, _):
             base = n * unroll
@@ -466,7 +505,7 @@
     first.from_right(2)
     lay_tokens()
     first.rest(0)
-    loads[1].wait()
+    late_loads[0].wait()
     convolve(field_one, True, conv_one_ref, 0, every, False)
     first.from_left(3)
     first.from_right(0)
@@ -503,15 +542,17 @@
     second.halo_out(0, k, 3)
     pass_first(second)
     second.halo_in(0)
+    second.from_left(3)
+    second.from_right(0)
+    late_loads[3].wait()
+    late_loads[4].wait()
     norm_one.settle()
     second.from_left(1)
     second.from_right(2)
-    second.from_left(3)
-    second.from_right(0)
     second.from_far(0)
     second.from_far(3)
     second.rest(0)
-    loads[2].wait()
+    late_loads[1].wait()
     norm_one.ready(0)
     slots = range(height + 2)
     normalise(second, 0, slots)
@@ -522,18 +563,25 @@
     second.halo_in(2)
     second.from_far(1)
     second.from_far(2)
+    middle, ends = range(1, height + 1), (0, height + 1)
     norm_one.ready(1)
-    second.rest(1)
-    normalise(second, 1, slots)
+    second.rest_rows(1, every)
+    normalise(second, 1, middle)
+    norm_one.ready(2)
+    second.rest_rows(2, every)
+    convolve(hidden_ref, False, conv_two_ref, 1, inner)
+    normalise(second, 2, middle)
     second.halo_in(3)
-    norm_one.ready(2)
-    second.rest(2)
-    normalise(second, 2, slots)
-    convolve(hidden_ref, False, conv_two_ref, 1, every)
+    second.rest_halo(1)
+    convolve(hidden_ref, False, conv_two_ref, 2, inner)
+    normalise(second, 1, ends)
+    second.rest_halo(2)
+    convolve(hidden_ref, False, conv_two_ref, 1, outer)
+    normalise(second, 2, ends)
     norm_one.ready(3)
     second.rest(3)
+    convolve(hidden_ref, False, conv_two_ref, 2, outer)
     normalise(second, 3, slots)
-    convolve(hidden_ref, False, conv_two_ref, 2, every)
     convolve(hidden_ref, False, conv_two_ref, 3, every)
     norm_one.sent()
 
@@ -544,27 +592,43 @@
     open_gather(third)
     norm_two.tell()
     pass_first(third)
+    late_loads[5].wait()
+    late_loads[6].wait()
     norm_two.settle()
     third.from_left(1)
     third.from_right(2)
     scale_two = coef_all[1, 0, 0:1, :]
     shift_two = coef_all[1, 0, 2:3, :]
-    for i in range(height):
-        v = conv_ref[i * width : (i + 1) * width, :] * scale_two + shift_two
-        features_ref[i] = (first.field[k, i + 1].astype(F32) + v).astype(BF16)
-
     vocab_here = head_hbm.shape[1]
     tiles = vocab_here // 128
 
+    def features_of(p, i):
+        d = lax.rem(k - p + num_cols, num_cols)
+        v = third.field[p, i].astype(F32) * coef_all[1, d, 0:1, :] + coef_all[1, d, 2:3, :]
+        return (first.field[p, i + 1].astype(F32) + v).astype(BF16)
+
+    def head_rows_of(q):
+        at = at_chip(q)
+        return head_ref[pl.ds(pl.multiple_of(at * 2 * lanes, 2 * lanes), 2 * lanes), :]
+
+    def own_logits():
+        for i in range(height):
+            made = [features_of(at_chip(0) * 2 + c, i) for c in range(2)]
+            early_ref[i] = jnp.dot(
+                jnp.concatenate(made, axis=1), head_rows_of(0), preferred_element_type=F32
+            )
+
     def all_features(i, to):
-        for p in range(num_cols):
-            d = lax.rem(k - p + num_cols, num_cols)
-            v = third.field[p, i].astype(F32) * coef_all[1, d, 0:1, :] + coef_all[1, d, 2:3, :]
-            v = first.field[p, i + 1].astype(F32) + v
-            rows_ref[to, :, p * lanes : (p + 1) * lanes] = v.astype(BF16)
-
-    def row_logits(to):
-        logits_ref[to] = jnp.dot(rows_ref[to], head_ref[...], preferred_element_type=F32)
+        for q in range(1, 4):
+            for c in range(2):
+                n = 2 * (q - 1) + c
+                rows_ref[to, :, n * lanes : (n + 1) * lanes] = features_of(at_chip(q) * 2 + c, i)
+
+    def row_logits(i, to):
+        weights = jnp.concatenate([head_rows_of(q) for q in range(1, 4)], axis=0)
+        logits_ref[to] = early_ref[i] + jnp.dot(
+            rows_ref[to], weights, preferred_element_type=F32
+        )
 
     def row_totals(i, to):
         most = logits_ref[to, :, 0:128]
@@ -591,28 +655,35 @@
     third.from_right(0)
     third.from_far(0)
     third.from_far(3)
+    for i in range(height):
+        v = conv_ref[i * width : (i + 1) * width, :] * scale_two + shift_two
+        features_ref[i] = (first.field[k, i + 1].astype(F32) + v).astype(BF16)
+    features_out = pltpu.make_async_copy(features_ref, features_hbm, load_sems.at[16])
+    features_out.start()
+    third.rest_rows(0, every)
+    late_loads[2].wait()
+    norm_two.ready(0)
+    own_logits()
     third.from_left(2)
     third.from_right(1)
-    for q in range(4):
+    for q in range(1, 4):
         third.rest_rows(q, (0, 3))
-    loads[3].wait()
-    for q in range(4):
         norm_two.ready(q)
     norm_two.sent()
     all_features(0, 0)
-    row_logits(0)
+    row_logits(0, 0)
     all_features(3, 1)
     third.from_far(1)
     third.from_far(2)
-    row_logits(1)
+    row_logits(3, 1)
     row_totals(0, 0)
-    for q in range(4):
+    for q in range(1, 4):
         third.rest_rows(q, (1, 2))
     all_features(1, 0)
-    row_logits(0)
+    row_logits(1, 0)
     row_totals(3, 1)
     all_features(2, 1)
-    row_logits(1)
+    row_logits(2, 1)
     row_totals(1, 0)
     row_totals(2, 1)
 
@@ -635,6 +706,7 @@
     for d in range(1, num_cols):
         exchange(d).wait_recv()
     totals_ref[...] = last_all[...]
+    features_out.wait()
 
     for copy in pending:
         copy.wait_send()
@@ -689,22 +761,18 @@
             jax.ShapeDtypeStruct((height, width, lanes), BF16),
             jax.ShapeDtypeStruct((num_cols, 3, height, 128), F32),
         ),
-        in_specs=[
-            in_vmem,
-            in_vmem,
-            in_vmem,
-            anywhere,
-            in_vmem,
-            anywhere,
-            in_vmem,
-            in_vmem,
-            anywhere,
-            in_vmem,
-            in_vmem,
-            anywhere,
-        ],
-        out_specs=(in_vmem, in_vmem),
+        in_specs=[anywhere] * 12,
+        out_specs=(anywhere, in_vmem),
         scratch_shapes=[
+            pltpu.VMEM((height, width), jnp.int32),
+            pltpu.VMEM((height, width), jnp.int32),
+            pltpu.VMEM((lines, 128), jnp.int32),
+            pltpu.VMEM((1, lanes), BF16),
+            pltpu.VMEM((1, lanes), F32),
+            pltpu.VMEM((1, lanes), F32),
+            pltpu.VMEM((1, lanes), F32),
+            pltpu.VMEM((1, lanes), F32),
+            pltpu.VMEM((height, width, lanes), BF16),
             pltpu.VMEM((vocab, lanes), BF16),
             pltpu.VMEM((vocab + 8, lanes), F32),
             pltpu.VMEM(conv_one.shape, BF16),
@@ -724,11 +792,12 @@
             pltpu.VMEM((2, 4, lanes), F32),
             pltpu.VMEM((2, num_cols, 4, lanes), F32),
             pltpu.VMEM((num_cols, height + 2, width, lanes), BF16),
-            pltpu.VMEM((2, width, num_cols * lanes), BF16),
+            pltpu.VMEM((2, width, (num_cols - 2) * lanes), BF16),
+            pltpu.VMEM((height, width, head_weight.shape[1]), F32),
             pltpu.VMEM((2, width, head_weight.shape[1]), F32),
             pltpu.VMEM((width // 128, 3, height, 128), F32),
             pltpu.VMEM((num_cols, 3, height, 128), F32),
-            pltpu.SemaphoreType.DMA((5,)),
+            pltpu.SemaphoreType.DMA((17,)),
             pltpu.SemaphoreType.DMA((3, 11, 4)),
             pltpu.SemaphoreType.DMA((3, 11, 4)),
             pltpu.SemaphoreType.DMA((2,)),

time: 69.5 us -> 67.1 us (0.965)
  Pallas kernels: 68.7 us -> 66.3 us
    pallas_call x1, Pallas kernels: 66.8 us -> 64.4 us  [local(): pl.pallas_call(functools.partial(kernel, num_rows, num_cols), name='denoi...]
where the time goes in v5:
time: 67.1 us; the launch traced here: 67 us
  Pallas kernels  66.3 us (99%)
    pallas_call x1, Pallas kernels, local(): pl.pallas_call(functools.partial(kernel, num_rows, num_cols), name='denoi...  64.4 us
    pallas_call x1, Pallas kernels, local(): pl.pallas_call(functools.partial(finish, num_cols), name='finish', out_sh...  1.9 us

profile of v5, /device:TPU:1, one launch (start us, length us, event | category | flops | bytes accessed | tf_op | source)
XLA Modules:
  0.0 67.0 jit_solution(6284054189998140223)
XLA Ops:
  0.6 64.4 %denoise.1 = (bf16[4,256,128]{2,1,0:T(8,128)(2,1)}, f32[8,3,4,128]{3,2,1,0:T(4,128)}) custom-call(s32[4,256]{1,0:T(4,128)} %ids_hbm.1, s32[4,256]{1,0:T(4,128)} %keep_hbm.1, s32[8,128]{1,0:T(8,128)} %bitcast.6, bf16[8192,128]{1,0:T(8,128)(2,1)} %table_hbm.1, bf16[1,128]{1,0:T(2,128)(2,1)} %bitcast.7, bf16[3,3,1024,128]{3,2,1,0:T(8,128)(2,1)} %conv_one_hbm.1, ...), custom_call_target="tpu_custom_call" | custom-call | tf_op jit(solution)/shard_map/denoise/pallas_call | solution.py:757
  65.1 1.9 %finish.1 = (bf16[4,256,128]{2,1,0:T(8,128)(2,1)}, f32[4,32]{1,0:T(4,128)}) custom-call(bf16[4,256,128]{2,1,0:T(8,128)(2,1)} %get-tuple-element.4.made_ref, f32[8,3,4,128]{3,2,1,0:T(4,128)} %get-tuple-element.5.last_all), custom_call_target="tpu_custom_call" | custom-call | tf_op jit(solution)/shard_map/finish/pallas_call | solution.py:828

commit v6 on v5

--- a/solution.py
+++ b/solution.py
@@ -279,8 +279,8 @@
     def at_chip(q):
         return lax.rem(chip + (0, chips - 1, 1, 2)[q], chips)
 
-    def normalise(gather, q, slots):
-        for c in range(2):
+    def normalise(gather, q, slots, cores=(0, 1)):
+        for c in cores:
             owner = at_chip(q) * 2 + c
             d = lax.rem(k - owner + num_cols, num_cols)
             scale = coef_all[0, d, 0:1, :]
@@ -528,8 +528,10 @@
     convolve(field_one, True, conv_one_ref, 1, outer)
     first.rest_halo(2)
     convolve(field_one, True, conv_one_ref, 2, outer)
-    first.rest(3)
-    convolve(field_one, True, conv_one_ref, 3, every)
+    first.rest_rows(3, every)
+    convolve(field_one, True, conv_one_ref, 3, inner)
+    first.rest_halo(3)
+    convolve(field_one, True, conv_one_ref, 3, outer)
 
     second = Gather(1, field_two, True)
     norm_one = Norm(0, gain_one_ref, bias_one_ref)
@@ -564,24 +566,28 @@
     second.from_far(1)
     second.from_far(2)
     middle, ends = range(1, height + 1), (0, height + 1)
+    mine_only, other_only = (core,), (1 - core,)
     norm_one.ready(1)
+    normalise(second, 1, middle, mine_only)
+    norm_one.ready(2)
+    normalise(second, 2, middle, mine_only)
     second.rest_rows(1, every)
-    normalise(second, 1, middle)
-    norm_one.ready(2)
+    normalise(second, 1, middle, other_only)
     second.rest_rows(2, every)
     convolve(hidden_ref, False, conv_two_ref, 1, inner)
-    normalise(second, 2, middle)
+    normalise(second, 2, middle, other_only)
     second.halo_in(3)
+    norm_one.ready(3)
     second.rest_halo(1)
+    normalise(second, 1, ends)
     convolve(hidden_ref, False, conv_two_ref, 2, inner)
-    normalise(second, 1, ends)
+    normalise(second, 3, slots, mine_only)
     second.rest_halo(2)
+    normalise(second, 2, ends)
     convolve(hidden_ref, False, conv_two_ref, 1, outer)
-    normalise(second, 2, ends)
-    norm_one.ready(3)
     second.rest(3)
+    normalise(second, 3, slots, other_only)
     convolve(hidden_ref, False, conv_two_ref, 2, outer)
-    normalise(second, 3, slots)
     convolve(hidden_ref, False, conv_two_ref, 3, every)
     norm_one.sent()
 

time: 67.1 us -> 67 us (level)
  no operation moved by 1% of the time
where the time goes in v6:
time: 67 us; the launch traced here: 66.9 us
  Pallas kernels  66.3 us (99%)
    pallas_call x1, Pallas kernels, local(): pl.pallas_call(functools.partial(kernel, num_rows, num_cols), name='denoi...  64.4 us
    pallas_call x1, Pallas kernels, local(): pl.pallas_call(functools.partial(finish, num_cols), name='finish', out_sh...  1.9 us

profile of v6, /device:TPU:1, one launch (start us, length us, event | category | flops | bytes accessed | tf_op | source)
XLA Modules:
  0.0 66.9 jit_solution(10462877351263186393)
XLA Ops:
  0.6 64.4 %denoise.1 = (bf16[4,256,128]{2,1,0:T(8,128)(2,1)}, f32[8,3,4,128]{3,2,1,0:T(4,128)}) custom-call(s32[4,256]{1,0:T(4,128)} %ids_hbm.1, s32[4,256]{1,0:T(4,128)} %keep_hbm.1, s32[8,128]{1,0:T(8,128)} %bitcast.6, bf16[8192,128]{1,0:T(8,128)(2,1)} %table_hbm.1, bf16[1,128]{1,0:T(2,128)(2,1)} %bitcast.7, bf16[3,3,1024,128]{3,2,1,0:T(8,128)(2,1)} %conv_one_hbm.1, ...), custom_call_target="tpu_custom_call" | custom-call | tf_op jit(solution)/shard_map/denoise/pallas_call | solution.py:763
  65.0 1.9 %finish.1 = (bf16[4,256,128]{2,1,0:T(8,128)(2,1)}, f32[4,32]{1,0:T(4,128)}) custom-call(bf16[4,256,128]{2,1,0:T(8,128)(2,1)} %get-tuple-element.4.made_ref, f32[8,3,4,128]{3,2,1,0:T(4,128)} %get-tuple-element.5.last_all), custom_call_target="tpu_custom_call" | custom-call | tf_op jit(solution)/shard_map/finish/pallas_call | solution.py:834
